TPU v7x, 32 devices: a whole 2x2x4 slice. The times are simulated.
32 devices in a mesh: part: 4 (over x, y), fsdp: 8 (over z, core).
Axes of the slice: x: 2, y: 2, z: 4, core: 2. Of those that a mesh axis runs over, the one named last changes fastest.
Arguments:
- acts_in: bfloat16 [2, 65536, 768], P(None, ('part', 'fsdp')), parts along dimension 1
- cot_out: bfloat16 [2, 65536, 768], P(None, ('part', 'fsdp')), parts along dimension 1
- lengths: int32 [2, 32], P(None, ('part', 'fsdp')), parts along dimension 1
- w_up: bfloat16 [2, 768, 3072], replicated
- w_down: bfloat16 [2, 3072, 768], replicated
Outputs:
- output 1: float32 [8, 768, 3072], P('part', 'fsdp'), parts along dimension 0
- output 2: float32 [8, 3072, 768], P('part', 'fsdp'), parts along dimension 0
There are 4 independent parts. A program takes and returns all parts, laid end to end along the dimension named above; an argument that names none is the same for every part.
All inputs are finite; a program needn't handle non-finite values.
Results may differ from a plain program's by a relative error of at most 0.00977007.
Values are sent between devices in bfloat16 or wider.
A program may use at most 1 GiB of HBM per device.

v0:
```python
import jax
import jax.numpy as jnp
from jax import lax
from jax.sharding import PartitionSpec as P

CONTRACT_LAST = (((1,), (1,)), ((), ()))
CONTRACT_FIRST = (((0,), (0,)), ((), ()))


def gelu_fwd(h_wide):
    return jax.nn.gelu(h_wide, approximate=True)


def gelu_back(h_wide, da_val):
    return jax.vjp(gelu_fwd, h_wide)[1](da_val)[0]


def solution(mesh):
    def local_step(acts_in, cot_out, lengths, w_up, w_down):
        micro, tok_rows, _ = acts_in.shape
        layers = w_up.shape[0]
        keep_mask = (jnp.arange(tok_rows)[None, :] < lengths).astype(jnp.bfloat16)
        acc_up = [None] * layers
        acc_down = [None] * layers
        for k_idx in range(micro):
            x_cur = acts_in[k_idx]
            saved = []
            for layer_idx in range(layers):
                h_val = jnp.dot(x_cur, w_up[layer_idx], preferred_element_type=jnp.float32).astype(jnp.bfloat16)
                a_val = gelu_fwd(h_val.astype(jnp.float32)).astype(jnp.bfloat16)
                y_val = jnp.dot(a_val, w_down[layer_idx], preferred_element_type=jnp.float32).astype(jnp.bfloat16)
                saved.append((x_cur, h_val, a_val))
                x_cur = (x_cur.astype(jnp.float32) + y_val.astype(jnp.float32)).astype(jnp.bfloat16)
            dx_cur = cot_out[k_idx] * keep_mask[k_idx][:, None]
            for layer_idx in reversed(range(layers)):
                x_prev, h_val, a_val = saved[layer_idx]
                da_val = lax.dot_general(dx_cur, w_down[layer_idx], CONTRACT_LAST, preferred_element_type=jnp.float32)
                dh_val = gelu_back(h_val.astype(jnp.float32), da_val).astype(jnp.bfloat16)
                grad_down = lax.dot_general(a_val, dx_cur, CONTRACT_FIRST, preferred_element_type=jnp.float32)
                grad_up = lax.dot_general(x_prev, dh_val, CONTRACT_FIRST, preferred_element_type=jnp.float32)
                if layer_idx > 0:
                    dx_back = lax.dot_general(dh_val, w_up[layer_idx], CONTRACT_LAST, preferred_element_type=jnp.float32)
                    dx_cur = (dx_cur.astype(jnp.float32) + dx_back).astype(jnp.bfloat16)
                shard_down = lax.psum_scatter(grad_down, "fsdp", scatter_dimension=0, tiled=True)
                shard_up = lax.psum_scatter(grad_up, "fsdp", scatter_dimension=0, tiled=True)
                acc_down[layer_idx] = shard_down if acc_down[layer_idx] is None else acc_down[layer_idx] + shard_down
                acc_up[layer_idx] = shard_up if acc_up[layer_idx] is None else acc_up[layer_idx] + shard_up
        return jnp.stack(acc_up), jnp.stack(acc_down)

    act_spec = P(None, ("part", "fsdp"), None)
    grad_spec = P("part", "fsdp", None)
    return jax.shard_map(local_step, mesh=mesh, in_specs=(act_spec, act_spec, P(None, ("part", "fsdp")), P(), P()), out_specs=(grad_spec, grad_spec), check_vma=False)
```

profile of v0, /device:TPU:16, one launch (start us, length us, event | category | flops | bytes accessed | tf_op | source)
XLA Modules:
  0.0 626.4 jit_solution(6436901650848318017)
XLA Ops:
  7.2 15.7 %convolution_convert_fusion.3 = bf16[2048,3072]{1,0:T(8,128)(2,1)} fusion(bf16[2,768,3072]{2,1,0:T(8,128)(2,1)} %param.8, bf16[2,2048,768]{2,1,0:T(8,128)(2,1)} %param.5), kind=kOutput, calls=%fused_computation.67 | convolution fusion | flops 9669967872 | bytes 20447232 | tf_op jit(solution)/shard_map/dot_general | solution.py:29
  22.9 12.9 %convolution_convert_fusion.1 = bf16[2048,3072]{1,0:T(8,128)(2,1)} fusion(bf16[2,768,3072]{2,1,0:T(8,128)(2,1)S(1)} %copy-done.5, bf16[2,2048,768]{2,1,0:T(8,128)(2,1)S(1)} %copy-done.6), kind=kOutput, calls=%fused_computation.65 | convolution fusion | flops 9669967872 | bytes 20447232 | tf_op jit(solution)/shard_map/dot_general | solution.py:29
  36.5 20.5 %add_convert_fusion.3 = bf16[2048,768]{1,0:T(8,128)(2,1)S(1)} fusion(bf16[2,3072,768]{2,1,0:T(8,128)(2,1)} %param.9, bf16[2,2048,768]{2,1,0:T(8,128)(2,1)} %param.5, bf16[2048,3072]{1,0:T(8,128)(2,1)} %convolution_convert_fusion.3), kind=kOutput, calls=%fused_computation.72 | convolution fusion | flops 9734455296 | bytes 23592960 | tf_op jit(solution)/shard_map/dot_general | solution.py:31
  57.1 20.3 %add_convert_fusion.1 = bf16[2048,768]{1,0:T(8,128)(2,1)S(1)} fusion(bf16[2,3072,768]{2,1,0:T(8,128)(2,1)} %param.9, bf16[2,2048,768]{2,1,0:T(8,128)(2,1)} %param.5, bf16[2048,3072]{1,0:T(8,128)(2,1)} %convolution_convert_fusion.1), kind=kOutput, calls=%fused_computation.70 | convolution fusion | flops 9734455296 | bytes 23592960 | tf_op jit(solution)/shard_map/dot_general | solution.py:31
  77.4 12.9 %convolution_convert_fusion = bf16[2048,3072]{1,0:T(8,128)(2,1)} fusion(bf16[2048,768]{1,0:T(8,128)(2,1)S(1)} %add_convert_fusion.1, bf16[2,768,3072]{2,1,0:T(8,128)(2,1)S(1)} %copy-done.5), kind=kOutput, calls=%fused_computation.64 | convolution fusion | flops 9669967872 | bytes 20447232 | tf_op jit(solution)/shard_map/dot_general | solution.py:29
  90.3 13.0 %convolution_convert_fusion.2 = bf16[2048,3072]{1,0:T(8,128)(2,1)} fusion(bf16[2048,768]{1,0:T(8,128)(2,1)S(1)} %add_convert_fusion.3, bf16[2,768,3072]{2,1,0:T(8,128)(2,1)S(1)} %copy-done.5), kind=kOutput, calls=%fused_computation.66 | convolution fusion | flops 9669967872 | bytes 20447232 | tf_op jit(solution)/shard_map/dot_general | solution.py:29
  103.3 28.6 %fusion.12 = bf16[2048,3072]{1,0:T(8,128)(2,1)} fusion(bf16[2048,3072]{1,0:T(8,128)(2,1)} %convolution_convert_fusion.2, bf16[2,3072,768]{2,1,0:T(8,128)(2,1)} %param.9, bf16[2,2048,768]{2,1,0:T(8,128)(2,1)} %param.6, bf16[2048]{0:T(1024)(128)(2,1)S(1)} %get-tuple-element.7), kind=kOutput, calls=%fused_computation.32 | convolution fusion | flops 9797369856 | bytes 33034240 | tf_op jit(solution)/shard_map/dot_general | solution.py:37
  131.8 15.7 %fusion.156 = f32[768,3072]{1,0:T(8,128)} fusion(bf16[2048,768]{1,0:T(8,128)(2,1)S(1)} %add_convert_fusion.3, bf16[2048,3072]{1,0:T(8,128)(2,1)} %fusion.12), kind=kOutput, calls=%fused_computation.158 | convolution fusion | flops 9663676416 | bytes 25165824 | tf_op jit(solution)/shard_map/dot_general | solution.py:40
  147.6 27.3 %fusion.6 = bf16[2048,3072]{1,0:T(8,128)(2,1)} fusion(bf16[2048,3072]{1,0:T(8,128)(2,1)} %convolution_convert_fusion, bf16[2,3072,768]{2,1,0:T(8,128)(2,1)S(1)} %bitcast.104, bf16[2,2048,768]{2,1,0:T(8,128)(2,1)} %param.6, bf16[2048]{0:T(1024)(128)(2,1)S(1)} %copy-done.2), kind=kOutput, calls=%fused_computation.26 | convolution fusion | flops 9797369856 | bytes 33034240 | tf_op jit(solution)/shard_map/dot_general | solution.py:37
  174.8 16.9 %convolution_add_fusion.1 = f32[768,3072]{1,0:T(8,128)} fusion(f32[768,3072]{1,0:T(8,128)} %fusion.156, bf16[2048,768]{1,0:T(8,128)(2,1)S(1)} %add_convert_fusion.1, bf16[2048,3072]{1,0:T(8,128)(2,1)} %fusion.6), kind=kOutput, calls=%fused_computation.76 | convolution fusion | flops 9666035712 | bytes 34603008 | tf_op jit(solution)/shard_map/dot_general | solution.py:40
  191.8 14.8 %add_convert_fusion = bf16[2048,768]{1,0:T(8,128)(2,1)S(1)} fusion(bf16[2048,3072]{1,0:T(8,128)(2,1)} %fusion.6, bf16[2,768,3072]{2,1,0:T(8,128)(2,1)} %param.8, bf16[2,2048,768]{2,1,0:T(8,128)(2,1)} %param.6, bf16[2048]{0:T(1024)(128)(2,1)S(1)} %copy-done.2), kind=kOutput, calls=%fused_computation.69 | convolution fusion | flops 9669967872 | bytes 23597056 | tf_op jit(solution)/shard_map/dot_general | solution.py:42
  206.6 15.9 %add_convert_fusion.2 = bf16[2048,768]{1,0:T(8,128)(2,1)} fusion(bf16[2048,3072]{1,0:T(8,128)(2,1)} %fusion.12, bf16[2,768,3072]{2,1,0:T(8,128)(2,1)} %param.8, bf16[2,2048,768]{2,1,0:T(8,128)(2,1)} %param.6, bf16[2048]{0:T(1024)(128)(2,1)S(1)} %get-tuple-element.7), kind=kOutput, calls=%fused_computation.71 | convolution fusion | flops 9669967872 | bytes 23597056 | tf_op jit(solution)/shard_map/dot_general | solution.py:42
  222.5 43.1 %fusion.44 = f32[3072,768]{1,0:T(8,128)} fusion(bf16[2048,3072]{1,0:T(8,128)(2,1)} %convolution_convert_fusion.3, bf16[2048,768]{1,0:T(8,128)(2,1)} %add_convert_fusion.2, bf16[2,3072,768]{2,1,0:T(8,128)(2,1)} %param.9, bf16[2,2048,768]{2,1,0:T(8,128)(2,1)} %param.5), kind=kOutput, calls=%fused_computation.62 | convolution fusion | flops 19459473408 | bytes 33030144 | tf_op jit(solution)/shard_map/dot_general | solution.py:40
  265.6 42.4 %add_bitcast_fusion = f32[768,3072]{0,1:T(8,128)} fusion(f32[3072,768]{1,0:T(8,128)} %fusion.44, bf16[2048,3072]{1,0:T(8,128)(2,1)} %convolution_convert_fusion.1, bf16[2048,768]{1,0:T(8,128)(2,1)S(1)} %add_convert_fusion, bf16[2,3072,768]{2,1,0:T(8,128)(2,1)} %param.9, bf16[2,2048,768]{2,1,0:T(8,128)(2,1)} %param.5), kind=kOutput, calls=%fused_computation.68 | convolution fusion | flops 19461832704 | bytes 42467328 | tf_op jit(solution)/shard_map/dot_general | solution.py:40
  308.0 9.6 %copy.12 = f32[768,3072]{1,0:T(8,128)} copy(f32[768,3072]{0,1:T(8,128)} %add_bitcast_fusion) | data formatting | bytes 18874368
  317.7 21.4 %fusion.40 = f32[3072,768]{1,0:T(8,128)} fusion(bf16[2048,3072]{1,0:T(8,128)(2,1)} %convolution_convert_fusion, bf16[2,2048,768]{2,1,0:T(8,128)(2,1)} %param.6, bf16[2048]{0:T(1024)(128)(2,1)S(1)} %copy-done.3), kind=kOutput, calls=%fused_computation.60 | convolution fusion | flops 9728163840 | bytes 25169920 | tf_op jit(solution)/shard_map/dot_general | solution.py:39
  339.1 22.4 %fusion.52 = f32[3072,768]{1,0:T(8,128)} fusion(f32[3072,768]{1,0:T(8,128)} %fusion.40, bf16[2048,3072]{1,0:T(8,128)(2,1)} %convolution_convert_fusion.2, bf16[2,2048,768]{2,1,0:T(8,128)(2,1)} %param.6, bf16[2048]{0:T(1024)(128)(2,1)S(1)} %copy-done.1), kind=kOutput, calls=%fused_computation.74 | convolution fusion | flops 9730523136 | bytes 34607104 | tf_op jit(solution)/shard_map/dot_general | solution.py:39
  361.6 17.7 %fusion.153 = f32[3072,768]{1,0:T(8,128)S(1)} fusion(bf16[2048,768]{1,0:T(8,128)(2,1)} %add_convert_fusion.2, bf16[2048,3072]{1,0:T(8,128)(2,1)} %convolution_convert_fusion.3), kind=kOutput, calls=%fused_computation.157 | convolution fusion | flops 9726590976 | bytes 25165824 | tf_op jit(solution)/shard_map/dot_general | solution.py:39
  379.3 20.1 %convolution_add_fusion = f32[3072,768]{1,0:T(8,128)} fusion(f32[3072,768]{1,0:T(8,128)S(1)} %fusion.153, bf16[2048,768]{1,0:T(8,128)(2,1)S(1)} %add_convert_fusion, bf16[2048,3072]{1,0:T(8,128)(2,1)} %convolution_convert_fusion.1), kind=kOutput, calls=%fused_computation.75 | convolution fusion | flops 9728950272 | bytes 34603008 | tf_op jit(solution)/shard_map/dot_general | solution.py:39
  399.5 2.9 copy.15
  402.4 13.5 %reduce-scatter.13.cloned.1.call-done = f32[96,3072]{1,0:T(8,128)} async-done(((f32[768,3072]{1,0:T(8,128)}), f32[96,3072]{1,0:T(8,128)}) %reduce-scatter.13.cloned.1.call-update) | async-done | bytes 1179664
  423.1 93.2 %reduce-scatter.11.cloned.1.call-done = f32[384,768]{1,0:T(8,128)} async-done(((f32[3072,768]{1,0:T(8,128)}), f32[384,768]{1,0:T(8,128)}) %reduce-scatter.11.cloned.1.call-update) | async-done | bytes 1179664 | tf_op jit(solution)/shard_map/reduce_scatter | solution.py:44
  516.3 100.2 %reduce-scatter.9.cloned.1.call-done = f32[384,768]{1,0:T(8,128)} async-done(((f32[3072,768]{1,0:T(8,128)}), f32[384,768]{1,0:T(8,128)}) %reduce-scatter.9.cloned.1.call-update) | async-done | bytes 1179664 | tf_op jit(solution)/shard_map/reduce_scatter | solution.py:44
  616.4 3.2 pad_maximum_fusion.1
  (35 shorter events, 8.2 us)
Async XLA Ops:
  7.2 392.4 %reduce-scatter.15.cloned.1.call-start = ((), (), s32[]{:S(2)}) async-start(), calls=%async_computation.7 | async-start | bytes 10616832
  7.2 15.7 %copy-start.5 = (bf16[2,768,3072]{2,1,0:T(8,128)(2,1)S(1)}, bf16[2,768,3072]{2,1,0:T(8,128)(2,1)}, u32[]{:S(2)}) copy-start(bf16[2,768,3072]{2,1,0:T(8,128)(2,1)} %param.8) | copy-start | bytes 28311556
  7.2 15.7 %copy-start.6 = (bf16[2,2048,768]{2,1,0:T(8,128)(2,1)S(1)}, bf16[2,2048,768]{2,1,0:T(8,128)(2,1)}, u32[]{:S(2)}) copy-start(bf16[2,2048,768]{2,1,0:T(8,128)(2,1)} %param.5) | copy-start | bytes 18874372
  22.9 12.9 %copy-start.4 = (s32[2,1]{0,1:T(1,128)S(1)}, s32[2,1]{0,1:T(1,128)}, u32[]{:S(2)}) copy-start(s32[2,1]{0,1:T(1,128)} %param.7) | copy-start | bytes 28
  36.5 170.1 %copy-start = (bf16[2048]{0:T(1024)(128)(2,1)}, bf16[2048]{0:T(1024)(128)(2,1)S(1)}, u32[]{:S(2)}) copy-start(bf16[2048]{0:T(1024)(128)(2,1)S(1)} %get-tuple-element.7) | copy-start | bytes 12292
  90.3 57.2 %slice-start = ((s8[9437184]{0:T(1024)(128)(4,1)}), s8[1048576]{0:T(1024)(128)(4,1)S(1)}, s32[]{:S(2)}) async-start(s8[9437184]{0:T(1024)(128)(4,1)} %bitcast.103), calls=%async_computation.8 | async-start | bytes 2097152
  103.3 44.3 %slice-start.1 = ((s8[9437184]{0:T(1024)(128)(4,1)}), s8[4194304]{0:T(1024)(128)(4,1)S(1)}, s32[]{:S(2)}) async-start(s8[9437184]{0:T(1024)(128)(4,1)} %bitcast.103), calls=%async_computation.9 | async-start | bytes 8388608
  103.3 44.3 %slice-start.2 = ((s8[9437184]{0:T(1024)(128)(4,1)}), s8[4194304]{0:T(1024)(128)(4,1)S(1)}, s32[]{:S(2)}) async-start(s8[9437184]{0:T(1024)(128)(4,1)} %bitcast.103), calls=%async_computation.10 | async-start | bytes 8388608
  131.8 15.7 %copy-start.2 = (bf16[2048]{0:T(1024)(128)(2,1)S(1)}, bf16[2048]{0:T(1024)(128)(2,1)}, u32[]{:S(2)}) copy-start(bf16[2048]{0:T(1024)(128)(2,1)} %get-tuple-element.6) | copy-start | bytes 12292
  191.7 224.2 %reduce-scatter.13.cloned.1.call-start = ((), (), s32[]{:S(2)}) async-start(), calls=%async_computation.6 | async-start | bytes 10616832
  308.0 9.7 %copy-start.3 = (bf16[2048]{0:T(1024)(128)(2,1)S(1)}, bf16[2048]{0:T(1024)(128)(2,1)}, u32[]{:S(2)}) copy-start(bf16[2048]{0:T(1024)(128)(2,1)} %get-tuple-element.6) | copy-start | bytes 12292
  317.7 21.5 %copy-start.1 = (bf16[2048]{0:T(1024)(128)(2,1)S(1)}, bf16[2048]{0:T(1024)(128)(2,1)}, u32[]{:S(2)}) copy-start(bf16[2048]{0:T(1024)(128)(2,1)} %copy-done) | copy-start | bytes 12292
  317.7 198.6 %reduce-scatter.11.cloned.1.call-start = ((), (), s32[]{:S(2)}) async-start(), calls=%async_computation.5 | async-start | bytes 10616832 | tf_op jit(solution)/shard_map/reduce_scatter | solution.py:44
  361.6 254.9 %reduce-scatter.9.cloned.1.call-start = ((), (), s32[]{:S(2)}) async-start(), calls=%async_computation.4 | async-start | bytes 10616832 | tf_op jit(solution)/shard_map/reduce_scatter | solution.py:44
Sparse Core Ops, SparseCore 0:
  191.8 98.0 reduce-scatter.14
  317.8 98.0 reduce-scatter.12
  418.2 97.9 reduce-scatter.10
  518.4 97.9 reduce-scatter.8
where the time goes:
time: 636 us; the launch traced here: 626 us
  matrix products  382 us (60%)
  waiting for transfers between devices  207 us (33%)
  local copies, waits for them, and re-layouts  18.2 us (3%)
  between operations  14.1 us (2%)
    reduce_scatter x2, waiting for transfers between devices, local_step(): lax.psum_scatter(grad_down, 'fsdp', scatter_dimension=0, tiled=True)  193 us
    dot_general x4, matrix products, local_step(): lax.dot_general(x_prev, dh_val, CONTRACT_FIRST, preferred_element_type=jn...  118 us
    dot_general x4, matrix products, local_step(): lax.dot_general(a_val, dx_cur, CONTRACT_FIRST, preferred_element_type=jnp...  81.7 us
    dot_general x2, matrix products, local_step(): lax.dot_general(dx_cur, w_down[layer_idx], CONTRACT_LAST, preferred_eleme...  55.8 us
    dot_general x4, matrix products, local_step(): jnp.dot(x_cur, w_up[layer_idx], preferred_element_type=jnp.float32)  54.4 us
    dot_general x2, matrix products, local_step(): jnp.dot(a_val, w_down[layer_idx], preferred_element_type=jnp.float32)  40.8 us
    dot_general x2, matrix products, local_step(): lax.dot_general(dh_val, w_up[layer_idx], CONTRACT_LAST, preferred_element...  30.7 us
    unnamed x24, local copies, waits for them, and re-layouts  17.6 us
  transfers between devices with their start and end apart: 4, of which 3 were waited for; matrix products, arithmetic and copies ran while one was open for 35% of the time, Pallas kernels for 0%

commit v1 on v0

v1 whole, which is shorter than its diff:
```python
import functools

import jax
import jax.numpy as jnp
from jax import lax
from jax.experimental import pallas as pl
from jax.experimental.pallas import tpu as pltpu
from jax.sharding import PartitionSpec as P

MESH = pl.DeviceIdType.MESH
F32 = jnp.float32
BF16 = jnp.bfloat16

C1 = 0.7978845608028654
K1 = C1 * 0.044715
K3 = 3.0 * K1

CHIPS = 4
HOP = 2
SLOTS = 8
PARTS = 4
SHIFT = 1


def dot(lhs, rhs, dims):
    return lax.dot_general(lhs, rhs, (dims, ((), ())), preferred_element_type=F32)


def gelu_parts(h_wide):
    sq = h_wide * h_wide
    th = jnp.tanh(h_wide * (C1 + K1 * sq))
    return sq, th, 0.5 + 0.5 * th


def kernel(unit, block, micro, len_s, x0_h, g_h, wu_h, wd_h, gu_h, gd_h,
           xv, rv, x_extra, w1v, w2v, own_u, own_v, in_u, in_v, sum_u, sum_v,
           rr_u, rr_v, rl_u, rl_v, out_u, out_v,
           x_sem, r_sem, w_sem, f_sem, t_send, t_recv, ds_sem, dr_sem,
           rs_u, rq_u, ls_u, lq_u, rs_v, rq_v, ls_v, lq_v,
           ou_sem, ov_sem, du_credit, dv_credit, ru_credit, lu_credit, rv_credit, lv_credit):
    toks, dim = x0_h.shape
    layers, _, ff = wu_h.shape
    tiles = toks // block
    wide = 2 * unit
    per_dev = ff // (2 * CHIPS)
    per_layer = ff // wide
    total = layers * per_layer

    me = lax.axis_index("fsdp")
    z = me // 2
    core = me % 2
    peer = z * 2 + (1 - core)
    at_end = (z == 0) | (z == CHIPS - 1)
    inward = jnp.where(z < CHIPS // 2, me + 2, me - 2)
    outward = jnp.where(z < CHIPS // 2, me - 2, me + 2)
    mine = jnp.where(at_end, tiles - SHIFT, tiles + SHIFT)

    def signal(sem, dev):
        pl.semaphore_signal(sem, inc=1, device_id={"fsdp": dev}, device_id_type=MESH)

    def remote(src, dst, ssem, rsem, dev):
        return pltpu.make_async_remote_copy(
            src_ref=src, dst_ref=dst, send_sem=ssem, recv_sem=rsem,
            device_id={"fsdp": dev}, device_id_type=MESH)

    barrier = pltpu.get_barrier_semaphore()
    signal(barrier, peer)

    @pl.when(z > 0)
    def _():
        signal(barrier, me - 2)

    @pl.when(z < CHIPS - 1)
    def _():
        signal(barrier, me + 2)

    def layer_of(m):
        return layers - 1 - m // per_layer

    def owner_of(m):
        return (1 + 3 * (m % per_layer)) % CHIPS

    def cols_of(m):
        base = 2 * per_dev * owner_of(m) + unit * ((m % per_layer) // CHIPS)
        return pl.multiple_of(base, unit), pl.multiple_of(base + per_dev, unit)

    def w_copies(m):
        slot = m % 2
        out = []
        for half, start in enumerate(cols_of(m)):
            span = pl.ds(start, unit)
            here = pl.ds(half * unit, unit)
            out.append(pltpu.make_async_copy(
                wu_h.at[layer_of(m), :, span], w1v.at[slot, :, here], w_sem.at[slot, half]))
            out.append(pltpu.make_async_copy(
                wd_h.at[layer_of(m), span, :], w2v.at[slot, here, :], w_sem.at[slot, 2 + half]))
        return out

    def rows_of(i):
        return pl.ds(pl.multiple_of(i * block, block), block)

    def x_copy(i):
        return pltpu.make_async_copy(x0_h.at[rows_of(i), :], xv.at[rows_of(i), :], x_sem.at[i])

    def r_copy(i):
        return pltpu.make_async_copy(g_h.at[rows_of(i), :], rv.at[rows_of(i), :], r_sem.at[i])

    def mask(i):
        per = tiles // micro
        left = len_s[i // per] - (i % per) * block
        r_val = rv[rows_of(i), :]
        row_ids = lax.broadcasted_iota(jnp.int32, r_val.shape, 0)
        rv[rows_of(i), :] = jnp.where(row_ids < left, r_val, jnp.zeros_like(r_val))

    def tile_copies(k, dev):
        src = rows_of(tiles - SHIFT + k)
        dst = rows_of(tiles + k)
        return [
            remote(xv.at[src, :], xv.at[dst, :], t_send.at[0, k], t_recv.at[0, k], dev),
            remote(rv.at[src, :], rv.at[dst, :], t_send.at[1, k], t_recv.at[1, k], dev),
        ]

    def forward(w1f, w2f, a_scr):
        width = ff // PARTS

        def w1_copy(part):
            cols = pl.ds(part * width, width)
            return pltpu.make_async_copy(wu_h.at[0, :, cols], w1f.at[:, cols], f_sem.at[part])

        w2_copy = pltpu.make_async_copy(wd_h.at[0], w2f, f_sem.at[PARTS])
        for k in range(SHIFT):
            @pl.when(at_end)
            def _():
                x_copy(tiles - SHIFT + k).start()
                r_copy(tiles - SHIFT + k).start()

        for i in range(tiles - SHIFT):
            x_copy(i).start()
            if i == 0:
                for part in range(PARTS):
                    w1_copy(part).start()
                w2_copy.start()
        for i in range(tiles - SHIFT):
            r_copy(i).start()

        @pl.when(~at_end)
        def _():
            for k in range(SHIFT):
                x_copy(tiles - SHIFT + k).start()
                r_copy(tiles - SHIFT + k).start()

        for cp in w_copies(0):
            cp.start()
        peers = 1 + jnp.where(z > 0, 1, 0) + jnp.where(z < CHIPS - 1, 1, 0)
        pl.semaphore_wait(barrier, peers)

        @pl.when(at_end)
        def _():
            for k in range(SHIFT):
                i = tiles - SHIFT + k
                x_copy(i).wait()
                r_copy(i).wait()
                mask(i)
                for cp in tile_copies(k, inward):
                    cp.start()

        def tile(i, first):
            @pl.when(i < tiles)
            def _():
                x_copy(i).wait()
                r_copy(i).wait()
                mask(i)

            for k in range(SHIFT):
                @pl.when(i == tiles + k)
                def _():
                    for cp in tile_copies(k, outward):
                        cp.wait_recv()
                    x_extra[k * block:(k + 1) * block, :] = xv[rows_of(i), :]

            x_val = xv[rows_of(i), :]
            for part in range(PARTS):
                cols = slice(part * width, (part + 1) * width)

                if first:
                    w1_copy(part).wait()
                h_val = dot(x_val, w1f[:, cols], ((1,), (0,))).astype(BF16).astype(F32)
                _, _, cdf = gelu_parts(h_val)
                a_scr[:, cols] = (h_val * cdf).astype(BF16)

            if first:
                w2_copy.wait()
            y_val = dot(a_scr[...], w2f[...], ((1,), (0,))).astype(BF16)
            xv[rows_of(i), :] = (x_val.astype(F32) + y_val.astype(F32)).astype(BF16)

        def rest(i, carry):
            tile(i, False)
            return carry

        tile(0, True)
        lax.fori_loop(1, mine, rest, 0)

        @pl.when(at_end)
        def _():
            for k in range(SHIFT):
                for cp in tile_copies(k, inward):
                    cp.wait_send()

    pl.run_scoped(
        forward,
        pltpu.VMEM((dim, ff), BF16), pltpu.VMEM((ff, dim), BF16), pltpu.VMEM((block, ff), BF16))

    def backward(dxa):
        def clear(i, carry):
            dxa[rows_of(i), :] = jnp.zeros((block, dim), F32)
            return carry

        lax.fori_loop(0, mine, clear, 0)

        def tile(m, i, back):
            slot = m % 2
            rows = rows_of(i)

            @pl.when(m == per_layer)
            def _():
                @pl.when(i < tiles)
                def _():
                    x_copy(i).wait()

                for k in range(SHIFT):
                    @pl.when(i == tiles + k)
                    def _():
                        xv[rows, :] = x_extra[k * block:(k + 1) * block, :]

                rv[rows, :] = (rv[rows, :].astype(F32) + dxa[rows, :]).astype(BF16)

            x_i, r_i = xv[rows, :], rv[rows, :]
            h_val = dot(x_i, w1v[slot], ((1,), (0,))).astype(BF16).astype(F32)
            da_val = dot(r_i, w2v[slot], ((1,), (1,)))
            sq, th, cdf = gelu_parts(h_val)
            a_val = (h_val * cdf).astype(BF16)
            slope = cdf + (h_val * (0.5 - 0.5 * (th * th))) * (C1 + K3 * sq)
            dh_val = (da_val * slope).astype(BF16)
            own_v[slot] += dot(a_val, r_i, ((0,), (0,))).reshape(own_v.shape[1:])
            own_u[slot] += dot(x_i, dh_val, ((0,), (0,))).reshape(own_u.shape[1:])
            if back:
                dxa[rows, :] += dot(dh_val, w1v[slot], ((1,), (1,)))

        def d_copies(m):
            slot = m % 2
            return (
                remote(own_u.at[slot, :, 1 - core], in_u.at[slot], ds_sem.at[0, slot], dr_sem.at[0, slot], peer),
                remote(own_v.at[slot, 1 - core], in_v.at[slot], ds_sem.at[1, slot], dr_sem.at[1, slot], peer),
            )

        def u_copy(m, zz, going, first):
            slot = m % SLOTS
            dst, ssem, qsem = (rr_u, rs_u, rq_u) if going > 0 else (rl_u, ls_u, lq_u)
            src = sum_u if first else dst
            part = pl.ds(zz + 1, CHIPS - 1 - zz) if going > 0 else pl.ds(0, zz)
            return remote(src.at[slot, part], dst.at[slot, part], ssem.at[slot], qsem.at[slot], me + 2 * going)

        def v_copy(m, going, first):
            slot = m % SLOTS
            dst, ssem, qsem = (rr_v, rs_v, rq_v) if going > 0 else (rl_v, ls_v, lq_v)
            src = sum_v if first else dst
            return remote(src.at[slot], dst.at[slot], ssem.at[slot], qsem.at[slot], me + 2 * going)

        def beyond(m, zz, going):
            return owner_of(m) > zz if going > 0 else owner_of(m) < zz

        def ends(zz, going):
            start, stop = (0, CHIPS - 1) if going > 0 else (CHIPS - 1, 0)
            return zz == start, zz == stop

        def turn(zz, going):
            return zz if going > 0 else CHIPS - 1 - zz

        def keeps(zz, going):
            return 2 * turn(zz, going) < CHIPS - 1

        def flow(m, zz, going):
            slot = m % SLOTS
            first, last = ends(zz, going)
            got, credit = (rr_u, ru_credit) if going > 0 else (rl_u, lu_credit)
            if not first:
                u_copy(m, zz - going, going, False).wait_recv()
                near = zz if keeps(zz, going) else zz + going
                lo, hi = (near, CHIPS) if going > 0 else (0, near + 1)
                if hi > lo:
                    got[slot, lo:hi] += sum_u[slot, lo:hi]
            if not last:
                @pl.when(m >= SLOTS)
                def _():
                    pl.semaphore_wait(credit, 1)

                u_copy(m, zz, going, first).start()

            got, credit = (rr_v, rv_credit) if going > 0 else (rl_v, lv_credit)
            if not first:
                @pl.when(beyond(m, zz - going, going))
                def _():
                    v_copy(m, going, False).wait_recv()

                @pl.when(beyond(m, zz - going if keeps(zz, going) else zz, going))
                def _():
                    got[slot] += sum_v[slot]

            if not last:
                @pl.when(beyond(m, zz, going))
                def _():
                    @pl.when(m >= SLOTS)
                    def _():
                        pl.semaphore_wait(credit, 1)

                    v_copy(m, going, first).start()

        def out_copies_u(m):
            slot = m % 2
            return [
                pltpu.make_async_copy(out_u.at[slot, :, pl.ds(half * unit, unit)],
                                      gu_h.at[layer_of(m), :, pl.ds(start, unit)], ou_sem.at[slot, half])
                for half, start in enumerate(cols_of(m))
            ]

        def out_copy_v(m):
            start = pl.multiple_of(unit * ((m % per_layer) // CHIPS), unit)
            return pltpu.make_async_copy(out_v, gd_h.at[layer_of(m), pl.ds(start, unit), :], ov_sem)

        def terms(zz, total_ref, right_ref, left_ref):
            if zz == 0:
                return total_ref, left_ref
            if zz == CHIPS - 1:
                return total_ref, right_ref
            return right_ref, left_ref

        def finish(m, zz):
            slot = m % SLOTS

            @pl.when(m >= 2)
            def _():
                for cp in out_copies_u(m - 2):
                    cp.wait()

            one, two = terms(zz, sum_u, rr_u, rl_u)
            out_u[m % 2] = one[slot, zz] + two[slot, zz]
            for cp in out_copies_u(m):
                cp.start()

            @pl.when(owner_of(m) == zz)
            def _():
                @pl.when(m >= CHIPS)
                def _():
                    out_copy_v(m - CHIPS).wait()

                one, two = terms(zz, sum_v, rr_v, rl_v)
                out_v[...] = one[slot] + two[slot]
                out_copy_v(m).start()

            again = m < total - SLOTS
            for going in (1, -1):
                first, last = ends(zz, going)
                if not last:
                    u_copy(m, zz, going, first).wait_send()

                    @pl.when(beyond(m, zz, going))
                    def _():
                        v_copy(m, going, first).wait_send()

                if not first:
                    @pl.when(again)
                    def _():
                        signal(ru_credit if going > 0 else lu_credit, me - 2 * going)

                    @pl.when(again & beyond(m, zz - going, going))
                    def _():
                        signal(rv_credit if going > 0 else lv_credit, me - 2 * going)

        def upto(k, n):
            late = n - total
            draining = jnp.where(late < k, total + 1 - HOP * (k - late), total)
            return jnp.maximum(jnp.where(n < total, n - HOP * k, draining), 0)

        def turns(k, n, body):
            def one(m, carry):
                body(m)
                return carry

            lax.fori_loop(upto(k, n - 1), upto(k, n), one, 0)

        def add_cores(m):
            for cp in d_copies(m):
                cp.wait_recv()
            sum_u[m % SLOTS] = own_u[m % 2, :, core] + in_u[m % 2]
            sum_v[m % SLOTS] = own_v[m % 2, core] + in_v[m % 2]
            for cp in d_copies(m):
                cp.wait_send()

            @pl.when(m < total - 2)
            def _():
                signal(du_credit, peer)
                signal(dv_credit, peer)

        def all_sums(n):
            turns(0, n, add_cores)
            for zz in range(CHIPS):
                @pl.when(z == zz)
                def _():
                    near, far = sorted((1, -1), key=lambda going: turn(zz, going))

                    def go(going):
                        turns(turn(zz, going), n, lambda m: flow(m, zz, going))

                    if turn(zz, near) == 0:
                        go(near)
                        go(far)
                    else:
                        @pl.when(n < total)
                        def _():
                            go(near)

                        go(far)

                        @pl.when(n >= total)
                        def _():
                            go(near)

                    turns(CHIPS - 1, n, lambda m: finish(m, zz))

        def step(n, carry):
            run = n < total

            @pl.when(run)
            def _():
                @pl.when(n + 1 < total)
                def _():
                    for cp in w_copies(n + 1):
                        cp.start()

                for cp in w_copies(n):
                    cp.wait()

                own_u[n % 2] = jnp.zeros(own_u.shape[1:], F32)
                own_v[n % 2] = jnp.zeros(own_v.shape[1:], F32)

                @pl.when(n == per_layer)
                def _():
                    for i in range(tiles - SHIFT):
                        x_copy(i).start()

                    @pl.when(~at_end)
                    def _():
                        for k in range(SHIFT):
                            x_copy(tiles - SHIFT + k).start()

            early = jnp.minimum((3 * n + 1) // 2, mine)

            def half(phase, c):
                lo = jnp.where(phase == 0, 0, early)
                hi = jnp.where(phase == 0, early, mine)

                def loop(cond, back):
                    @pl.when(cond)
                    def _():
                        def body(i, cc):
                            tile(n, i, back)
                            return cc

                        lax.fori_loop(lo, hi, body, 0)

                loop(run & (n < per_layer), True)
                loop(run & (n >= per_layer), False)

                @pl.when(run & (phase == 1))
                def _():
                    @pl.when(n >= 2)
                    def _():
                        pl.semaphore_wait(du_credit, 1)
                        pl.semaphore_wait(dv_credit, 1)

                    for cp in d_copies(n):
                        cp.start()

                @pl.when((phase == 0) == (early < mine))
                def _():
                    all_sums(n)

                return c

            lax.fori_loop(0, 2, half, 0)
            return carry

        lax.fori_loop(0, total + CHIPS, step, 0)

        for m in (total - 2, total - 1):
            for cp in out_copies_u(m):
                cp.wait()
        out_copy_v(total - CHIPS).wait()

    pl.run_scoped(backward, pltpu.VMEM(xv.shape, F32))


def gradients(x0, g, lengths, w_up, w_down, block, unit):
    toks, dim = x0.shape
    micro = lengths.shape[0]
    layers, _, ff = w_up.shape
    rows_u = dim // (2 * CHIPS)
    wide = 2 * unit
    tiles = toks // block
    held = toks + SHIFT * block
    dma = pltpu.SemaphoreType.DMA
    vm = pltpu.VMEM
    u_blk = (CHIPS, rows_u, wide)
    v_blk = (unit, dim)
    scratch = [
        vm((held, dim), BF16), vm((held, dim), BF16), vm((SHIFT * block, dim), BF16),
        vm((2, dim, wide), BF16), vm((2, wide, dim), BF16),
        vm((2, CHIPS, 2, rows_u, wide), F32), vm((2, 2) + v_blk, F32),
        vm((2,) + u_blk, F32), vm((2,) + v_blk, F32),
        vm((SLOTS,) + u_blk, F32), vm((SLOTS,) + v_blk, F32),
        vm((SLOTS,) + u_blk, F32), vm((SLOTS,) + v_blk, F32),
        vm((SLOTS,) + u_blk, F32), vm((SLOTS,) + v_blk, F32),
        vm((2, rows_u, wide), F32), vm(v_blk, F32),
        dma((tiles,)), dma((tiles,)), dma((2, 4)), dma((PARTS + 1,)),
        dma((2, SHIFT)), dma((2, SHIFT)), dma((2, 2)), dma((2, 2)),
    ] + [dma((SLOTS,))] * 8 + [dma((2, 2)), dma] + [pltpu.SemaphoreType.REGULAR] * 6
    any_space = pl.BlockSpec(memory_space=pl.ANY)
    return pl.pallas_call(
        functools.partial(kernel, unit, block, micro),
        out_shape=[
            jax.ShapeDtypeStruct((layers, rows_u, ff), F32),
            jax.ShapeDtypeStruct((layers, ff // (2 * CHIPS), dim), F32),
        ],
        in_specs=[pl.BlockSpec(memory_space=pltpu.SMEM)] + [any_space] * 4,
        out_specs=[any_space] * 2,
        scratch_shapes=scratch,
        compiler_params=pltpu.CompilerParams(
            collective_id=0, has_side_effects=True, vmem_limit_bytes=62 * 1024 * 1024),
        name="grads",
    )(lengths, x0, g, w_up, w_down)


def solution(mesh, block=512, unit=128):
    def local_step(acts_in, cot_out, lengths, w_up, w_down):
        micro, tok_rows, dim = acts_in.shape
        x0 = acts_in.reshape(micro * tok_rows, dim)
        g = cot_out.reshape(micro * tok_rows, dim)
        return gradients(x0, g, lengths.reshape(micro), w_up, w_down, block, unit)

    act_spec = P(None, ("part", "fsdp"), None)
    grad_spec = P("part", "fsdp", None)
    return jax.shard_map(
        local_step, mesh=mesh,
        in_specs=(act_spec, act_spec, P(None, ("part", "fsdp")), P(), P()),
        out_specs=(grad_spec, grad_spec), check_vma=False)
```

time: 636 us -> 426 us (0.67); the launches traced: 626 us -> 426 us
  Pallas kernels: 0 us -> 420 us
  matrix products: 382 us -> 0 us
  waiting for transfers between devices: 207 us -> 0 us
  between operations: 14.1 us -> 0.65 us
  local copies, waits for them, and re-layouts: 18.2 us -> 4.86 us
    pallas_call x0 -> x1, Pallas kernels: none -> 420 us  [gradients(): pl.pallas_call(functools.partial(kernel, unit, block, micro), out_shape=[...]
    dot_general x18 -> x0, matrix products: 382 us -> none  [the longest x4 118 us: local_step(): lax.dot_general(x_prev, dh_val, CONTRACT_FIRST, preferred_element_type=jn...]
    reduce_scatter x2 -> x0, waiting for transfers between devices: 193 us -> none  [local_step(): lax.psum_scatter(grad_down, 'fsdp', scatter_dimension=0, tiled=True)]
    unnamed x6 -> x0, waiting for transfers between devices: 13.6 us -> none
    unnamed x24 -> x4, local copies, waits for them, and re-layouts: 17.6 us -> 4.86 us
  transfers between devices with their start and end apart: 4 -> 0, of which waited for: 3 -> 0; matrix products, arithmetic and copies ran while one was open for 35% -> 0% of each run, Pallas kernels for 0% -> 0%
where the time goes in v1:
time: 426 us
  Pallas kernels  420 us (99%)
  local copies, waits for them, and re-layouts  4.86 us (1%)
    pallas_call x1, Pallas kernels, gradients(): pl.pallas_call(functools.partial(kernel, unit, block, micro), out_shape=[...  420 us

profile of v1, /device:TPU:16, one launch (start us, length us, event | category | flops | bytes accessed | tf_op | source)
XLA Modules:
  0.0 425.9 jit_solution(6598683074807111429)
XLA Ops:
  0.6 420.3 %grads.1 = (f32[2,96,3072]{2,1,0:T(8,128)}, f32[2,384,768]{2,1,0:T(8,128)}) custom-call(s32[2]{0:T(128)} %bitcast.5, bf16[4096,768]{1,0:T(8,128)(2,1)} %bitcast.3, bf16[4096,768]{1,0:T(8,128)(2,1)} %bitcast.4, bf16[2,768,3072]{2,1,0:T(8,128)(2,1)} %wu_h.1, bf16[2,3072,768]{2,1,0:T(8,128)(2,1)} %wd_h.1), custom_call_target="tpu_custom_call" | custom-call | tf_op jit(solution)/shard_map/grads/pallas_call | solution.py:528
  421.0 0.0 copy-start
  421.0 3.4 copy.9
  424.4 0.0 copy-done
  424.4 1.4 copy.10
Async XLA Ops:
  421.0 3.5 copy-start

commit v2 on v1

--- a/solution.py
+++ b/solution.py
@@ -18,8 +18,8 @@
 CHIPS = 4
 HOP = 2
 SLOTS = 8
+PIECES = 4
 PARTS = 4
-SHIFT = 1
 
 
 def dot(lhs, rhs, dims):
@@ -32,15 +32,17 @@
     return sq, th, 0.5 + 0.5 * th
 
 
-def kernel(unit, block, micro, len_s, x0_h, g_h, wu_h, wd_h, gu_h, gd_h,
-           xv, rv, x_extra, w1v, w2v, own_u, own_v, in_u, in_v, sum_u, sum_v,
+def kernel(unit, block, fblock, micro, len_s, x0_h, g_h, wu_h, wd_h, gu_h, gd_h,
+           xv, rv, w1v, w2v, own_u, own_v, in_u, in_v, sum_u, sum_v,
            rr_u, rr_v, rl_u, rl_v, out_u, out_v,
-           x_sem, r_sem, w_sem, f_sem, t_send, t_recv, ds_sem, dr_sem,
+           x_sem, r_sem, w_sem, f_sem, ds_sem, dr_sem,
            rs_u, rq_u, ls_u, lq_u, rs_v, rq_v, ls_v, lq_v,
            ou_sem, ov_sem, du_credit, dv_credit, ru_credit, lu_credit, rv_credit, lv_credit):
     toks, dim = x0_h.shape
     layers, _, ff = wu_h.shape
     tiles = toks // block
+    ftiles = toks // fblock
+    piece = unit // PIECES
     wide = 2 * unit
     per_dev = ff // (2 * CHIPS)
     per_layer = ff // wide
@@ -50,10 +52,6 @@
     z = me // 2
     core = me % 2
     peer = z * 2 + (1 - core)
-    at_end = (z == 0) | (z == CHIPS - 1)
-    inward = jnp.where(z < CHIPS // 2, me + 2, me - 2)
-    outward = jnp.where(z < CHIPS // 2, me - 2, me + 2)
-    mine = jnp.where(at_end, tiles - SHIFT, tiles + SHIFT)
 
     def signal(sem, dev):
         pl.semaphore_signal(sem, inc=1, device_id={"fsdp": dev}, device_id_type=MESH)
@@ -99,26 +97,21 @@
     def rows_of(i):
         return pl.ds(pl.multiple_of(i * block, block), block)
 
+    def frows_of(i):
+        return pl.ds(pl.multiple_of(i * fblock, fblock), fblock)
+
     def x_copy(i):
-        return pltpu.make_async_copy(x0_h.at[rows_of(i), :], xv.at[rows_of(i), :], x_sem.at[i])
+        return pltpu.make_async_copy(x0_h.at[frows_of(i), :], xv.at[frows_of(i), :], x_sem.at[i])
 
     def r_copy(i):
-        return pltpu.make_async_copy(g_h.at[rows_of(i), :], rv.at[rows_of(i), :], r_sem.at[i])
+        return pltpu.make_async_copy(g_h.at[frows_of(i), :], rv.at[frows_of(i), :], r_sem.at[i])
 
     def mask(i):
-        per = tiles // micro
-        left = len_s[i // per] - (i % per) * block
-        r_val = rv[rows_of(i), :]
+        per = ftiles // micro
+        left = len_s[i // per] - (i % per) * fblock
+        r_val = rv[frows_of(i), :]
         row_ids = lax.broadcasted_iota(jnp.int32, r_val.shape, 0)
-        rv[rows_of(i), :] = jnp.where(row_ids < left, r_val, jnp.zeros_like(r_val))
-
-    def tile_copies(k, dev):
-        src = rows_of(tiles - SHIFT + k)
-        dst = rows_of(tiles + k)
-        return [
-            remote(xv.at[src, :], xv.at[dst, :], t_send.at[0, k], t_recv.at[0, k], dev),
-            remote(rv.at[src, :], rv.at[dst, :], t_send.at[1, k], t_recv.at[1, k], dev),
-        ]
+        rv[frows_of(i), :] = jnp.where(row_ids < left, r_val, jnp.zeros_like(r_val))
 
     def forward(w1f, w2f, a_scr):
         width = ff // PARTS
@@ -128,57 +121,25 @@
             return pltpu.make_async_copy(wu_h.at[0, :, cols], w1f.at[:, cols], f_sem.at[part])
 
         w2_copy = pltpu.make_async_copy(wd_h.at[0], w2f, f_sem.at[PARTS])
-        for k in range(SHIFT):
-            @pl.when(at_end)
-            def _():
-                x_copy(tiles - SHIFT + k).start()
-                r_copy(tiles - SHIFT + k).start()
-
-        for i in range(tiles - SHIFT):
+        for i in range(ftiles):
             x_copy(i).start()
             if i == 0:
                 for part in range(PARTS):
                     w1_copy(part).start()
                 w2_copy.start()
-        for i in range(tiles - SHIFT):
+        for i in range(ftiles):
             r_copy(i).start()
-
-        @pl.when(~at_end)
-        def _():
-            for k in range(SHIFT):
-                x_copy(tiles - SHIFT + k).start()
-                r_copy(tiles - SHIFT + k).start()
 
         for cp in w_copies(0):
             cp.start()
         peers = 1 + jnp.where(z > 0, 1, 0) + jnp.where(z < CHIPS - 1, 1, 0)
         pl.semaphore_wait(barrier, peers)
 
-        @pl.when(at_end)
-        def _():
-            for k in range(SHIFT):
-                i = tiles - SHIFT + k
-                x_copy(i).wait()
-                r_copy(i).wait()
-                mask(i)
-                for cp in tile_copies(k, inward):
-                    cp.start()
-
         def tile(i, first):
-            @pl.when(i < tiles)
-            def _():
-                x_copy(i).wait()
-                r_copy(i).wait()
-                mask(i)
-
-            for k in range(SHIFT):
-                @pl.when(i == tiles + k)
-                def _():
-                    for cp in tile_copies(k, outward):
-                        cp.wait_recv()
-                    x_extra[k * block:(k + 1) * block, :] = xv[rows_of(i), :]
-
-            x_val = xv[rows_of(i), :]
+            x_copy(i).wait()
+            r_copy(i).wait()
+            mask(i)
+            x_val = xv[frows_of(i), :]
             for part in range(PARTS):
                 cols = slice(part * width, (part + 1) * width)
 
@@ -191,31 +152,25 @@
             if first:
                 w2_copy.wait()
             y_val = dot(a_scr[...], w2f[...], ((1,), (0,))).astype(BF16)
-            xv[rows_of(i), :] = (x_val.astype(F32) + y_val.astype(F32)).astype(BF16)
+            xv[frows_of(i), :] = (x_val.astype(F32) + y_val.astype(F32)).astype(BF16)
 
         def rest(i, carry):
             tile(i, False)
             return carry
 
         tile(0, True)
-        lax.fori_loop(1, mine, rest, 0)
-
-        @pl.when(at_end)
-        def _():
-            for k in range(SHIFT):
-                for cp in tile_copies(k, inward):
-                    cp.wait_send()
+        lax.fori_loop(1, ftiles, rest, 0)
 
     pl.run_scoped(
         forward,
-        pltpu.VMEM((dim, ff), BF16), pltpu.VMEM((ff, dim), BF16), pltpu.VMEM((block, ff), BF16))
+        pltpu.VMEM((dim, ff), BF16), pltpu.VMEM((ff, dim), BF16), pltpu.VMEM((fblock, ff), BF16))
 
     def backward(dxa):
         def clear(i, carry):
             dxa[rows_of(i), :] = jnp.zeros((block, dim), F32)
             return carry
 
-        lax.fori_loop(0, mine, clear, 0)
+        lax.fori_loop(0, tiles, clear, 0)
 
         def tile(m, i, back):
             slot = m % 2
@@ -223,15 +178,8 @@
 
             @pl.when(m == per_layer)
             def _():
-                @pl.when(i < tiles)
-                def _():
-                    x_copy(i).wait()
-
-                for k in range(SHIFT):
-                    @pl.when(i == tiles + k)
-                    def _():
-                        xv[rows, :] = x_extra[k * block:(k + 1) * block, :]
-
+                for k in range(block // fblock):
+                    x_copy(i * (block // fblock) + k).wait()
                 rv[rows, :] = (rv[rows, :].astype(F32) + dxa[rows, :]).astype(BF16)
 
             x_i, r_i = xv[rows, :], rv[rows, :]
@@ -253,18 +201,21 @@
                 remote(own_v.at[slot, 1 - core], in_v.at[slot], ds_sem.at[1, slot], dr_sem.at[1, slot], peer),
             )
 
-        def u_copy(m, zz, going, first):
+        def far_first(zz, going):
+            return list(range(CHIPS - 1, zz, -1)) if going > 0 else list(range(zz))
+
+        def u_copy(m, blk, going, first):
             slot = m % SLOTS
             dst, ssem, qsem = (rr_u, rs_u, rq_u) if going > 0 else (rl_u, ls_u, lq_u)
             src = sum_u if first else dst
-            part = pl.ds(zz + 1, CHIPS - 1 - zz) if going > 0 else pl.ds(0, zz)
-            return remote(src.at[slot, part], dst.at[slot, part], ssem.at[slot], qsem.at[slot], me + 2 * going)
-
-        def v_copy(m, going, first):
+            return remote(src.at[slot, blk], dst.at[slot, blk], ssem.at[blk, slot], qsem.at[blk, slot], me + 2 * going)
+
+        def v_copy(m, p, going, first):
             slot = m % SLOTS
             dst, ssem, qsem = (rr_v, rs_v, rq_v) if going > 0 else (rl_v, ls_v, lq_v)
             src = sum_v if first else dst
-            return remote(src.at[slot], dst.at[slot], ssem.at[slot], qsem.at[slot], me + 2 * going)
+            part = pl.ds(p * piece, piece)
+            return remote(src.at[slot, part], dst.at[slot, part], ssem.at[p, slot], qsem.at[p, slot], me + 2 * going)
 
         def beyond(m, zz, going):
             return owner_of(m) > zz if going > 0 else owner_of(m) < zz
@@ -282,38 +233,49 @@
         def flow(m, zz, going):
             slot = m % SLOTS
             first, last = ends(zz, going)
-            got, credit = (rr_u, ru_credit) if going > 0 else (rl_u, lu_credit)
-            if not first:
-                u_copy(m, zz - going, going, False).wait_recv()
-                near = zz if keeps(zz, going) else zz + going
-                lo, hi = (near, CHIPS) if going > 0 else (0, near + 1)
-                if hi > lo:
-                    got[slot, lo:hi] += sum_u[slot, lo:hi]
+            keep = keeps(zz, going)
+            got_u, credit_u = (rr_u, ru_credit) if going > 0 else (rl_u, lu_credit)
+            got_v, credit_v = (rr_v, rv_credit) if going > 0 else (rl_v, lv_credit)
+
             if not last:
                 @pl.when(m >= SLOTS)
                 def _():
-                    pl.semaphore_wait(credit, 1)
-
-                u_copy(m, zz, going, first).start()
-
-            got, credit = (rr_v, rv_credit) if going > 0 else (rl_v, lv_credit)
-            if not first:
-                @pl.when(beyond(m, zz - going, going))
-                def _():
-                    v_copy(m, going, False).wait_recv()
-
-                @pl.when(beyond(m, zz - going if keeps(zz, going) else zz, going))
-                def _():
-                    got[slot] += sum_v[slot]
-
+                    pl.semaphore_wait(credit_u, 1)
+
+                @pl.when((m >= SLOTS) & beyond(m, zz, going))
+                def _():
+                    pl.semaphore_wait(credit_v, 1)
+
+            def pass_u(blk):
+                if not first:
+                    u_copy(m, blk, going, False).wait_recv()
+                    if blk != zz or keep:
+                        got_u[slot, blk] += sum_u[slot, blk]
+                if blk != zz:
+                    u_copy(m, blk, going, first).start()
+
+            blocks = far_first(zz, going) + ([] if first else [zz])
+            pass_u(blocks[0])
             if not last:
                 @pl.when(beyond(m, zz, going))
                 def _():
-                    @pl.when(m >= SLOTS)
-                    def _():
-                        pl.semaphore_wait(credit, 1)
-
-                    v_copy(m, going, first).start()
+                    for p in range(PIECES):
+                        if not first:
+                            part = pl.ds(p * piece, piece)
+                            v_copy(m, p, going, False).wait_recv()
+                            got_v[slot, part] += sum_v[slot, part]
+                        v_copy(m, p, going, first).start()
+
+            if not first:
+                @pl.when(owner_of(m) == zz)
+                def _():
+                    for p in range(PIECES):
+                        v_copy(m, p, going, False).wait_recv()
+                    if keep:
+                        got_v[slot] += sum_v[slot]
+
+            for blk in blocks[1:]:
+                pass_u(blk)
 
         def out_copies_u(m):
             slot = m % 2
@@ -361,11 +323,13 @@
             for going in (1, -1):
                 first, last = ends(zz, going)
                 if not last:
-                    u_copy(m, zz, going, first).wait_send()
+                    for blk in far_first(zz, going):
+                        u_copy(m, blk, going, first).wait_send()
 
                     @pl.when(beyond(m, zz, going))
                     def _():
-                        v_copy(m, going, first).wait_send()
+                        for p in range(PIECES):
+                            v_copy(m, p, going, first).wait_send()
 
                 if not first:
                     @pl.when(again)
@@ -445,19 +409,13 @@
 
                 @pl.when(n == per_layer)
                 def _():
-                    for i in range(tiles - SHIFT):
+                    for i in range(ftiles):
                         x_copy(i).start()
 
-                    @pl.when(~at_end)
-                    def _():
-                        for k in range(SHIFT):
-                            x_copy(tiles - SHIFT + k).start()
-
-            early = jnp.minimum((3 * n + 1) // 2, mine)
 
             def half(phase, c):
-                lo = jnp.where(phase == 0, 0, early)
-                hi = jnp.where(phase == 0, early, mine)
+                lo = phase
+                hi = jnp.where(phase == 0, 1, tiles)
 
                 def loop(cond, back):
                     @pl.when(cond)
@@ -481,7 +439,7 @@
                     for cp in d_copies(n):
                         cp.start()
 
-                @pl.when((phase == 0) == (early < mine))
+                @pl.when(phase == 0)
                 def _():
                     all_sums(n)
 
@@ -500,20 +458,19 @@
     pl.run_scoped(backward, pltpu.VMEM(xv.shape, F32))
 
 
-def gradients(x0, g, lengths, w_up, w_down, block, unit):
+def gradients(x0, g, lengths, w_up, w_down, block, fblock, unit):
     toks, dim = x0.shape
     micro = lengths.shape[0]
     layers, _, ff = w_up.shape
     rows_u = dim // (2 * CHIPS)
     wide = 2 * unit
-    tiles = toks // block
-    held = toks + SHIFT * block
+    ftiles = toks // fblock
     dma = pltpu.SemaphoreType.DMA
     vm = pltpu.VMEM
     u_blk = (CHIPS, rows_u, wide)
     v_blk = (unit, dim)
     scratch = [
-        vm((held, dim), BF16), vm((held, dim), BF16), vm((SHIFT * block, dim), BF16),
+        vm((toks, dim), BF16), vm((toks, dim), BF16),
         vm((2, dim, wide), BF16), vm((2, wide, dim), BF16),
         vm((2, CHIPS, 2, rows_u, wide), F32), vm((2, 2) + v_blk, F32),
         vm((2,) + u_blk, F32), vm((2,) + v_blk, F32),
@@ -521,12 +478,11 @@
         vm((SLOTS,) + u_blk, F32), vm((SLOTS,) + v_blk, F32),
         vm((SLOTS,) + u_blk, F32), vm((SLOTS,) + v_blk, F32),
         vm((2, rows_u, wide), F32), vm(v_blk, F32),
-        dma((tiles,)), dma((tiles,)), dma((2, 4)), dma((PARTS + 1,)),
-        dma((2, SHIFT)), dma((2, SHIFT)), dma((2, 2)), dma((2, 2)),
-    ] + [dma((SLOTS,))] * 8 + [dma((2, 2)), dma] + [pltpu.SemaphoreType.REGULAR] * 6
+        dma((ftiles,)), dma((ftiles,)), dma((2, 4)), dma((PARTS + 1,)), dma((2, 2)), dma((2, 2)),
+    ] + [dma((CHIPS, SLOTS))] * 4 + [dma((PIECES, SLOTS))] * 4 + [dma((2, 2)), dma] + [pltpu.SemaphoreType.REGULAR] * 6
     any_space = pl.BlockSpec(memory_space=pl.ANY)
     return pl.pallas_call(
-        functools.partial(kernel, unit, block, micro),
+        functools.partial(kernel, unit, block, fblock, micro),
         out_shape=[
             jax.ShapeDtypeStruct((layers, rows_u, ff), F32),
             jax.ShapeDtypeStruct((layers, ff // (2 * CHIPS), dim), F32),
@@ -540,12 +496,12 @@
     )(lengths, x0, g, w_up, w_down)
 
 
-def solution(mesh, block=512, unit=128):
+def solution(mesh, block=1024, fblock=512, unit=128):
     def local_step(acts_in, cot_out, lengths, w_up, w_down):
         micro, tok_rows, dim = acts_in.shape
         x0 = acts_in.reshape(micro * tok_rows, dim)
         g = cot_out.reshape(micro * tok_rows, dim)
-        return gradients(x0, g, lengths.reshape(micro), w_up, w_down, block, unit)
+        return gradients(x0, g, lengths.reshape(micro), w_up, w_down, block, fblock, unit)
 
     act_spec = P(None, ("part", "fsdp"), None)
     grad_spec = P("part", "fsdp", None)

time: 426 us -> 390 us (0.915)
  Pallas kernels: 420 us -> 384 us
    pallas_call x1, Pallas kernels: 420 us -> 384 us  [gradients(): pl.pallas_call(functools.partial(kernel, unit, block, fblock, micro), out...]
where the time goes in v2:
time: 390 us
  Pallas kernels  384 us (98%)
  local copies, waits for them, and re-layouts  4.86 us (1%)
    pallas_call x1, Pallas kernels, gradients(): pl.pallas_call(functools.partial(kernel, unit, block, fblock, micro), out...  384 us

profile of v2, /device:TPU:16, one launch (start us, length us, event | category | flops | bytes accessed | tf_op | source)
XLA Modules:
  0.0 390.0 jit_solution(11478692307210972409)
XLA Ops:
  0.6 384.5 %grads.1 = (f32[2,96,3072]{2,1,0:T(8,128)}, f32[2,384,768]{2,1,0:T(8,128)}) custom-call(s32[2]{0:T(128)} %bitcast.5, bf16[4096,768]{1,0:T(8,128)(2,1)} %bitcast.3, bf16[4096,768]{1,0:T(8,128)(2,1)} %bitcast.4, bf16[2,768,3072]{2,1,0:T(8,128)(2,1)} %wu_h.1, bf16[2,3072,768]{2,1,0:T(8,128)(2,1)} %wd_h.1), custom_call_target="tpu_custom_call" | custom-call | tf_op jit(solution)/shard_map/grads/pallas_call | solution.py:484
  385.1 0.0 copy-start
  385.1 3.4 copy.9
  388.6 0.0 copy-done
  388.6 1.4 copy.10
Async XLA Ops:
  385.1 3.5 copy-start

commit v3 on v2

--- a/solution.py
+++ b/solution.py
@@ -33,14 +33,13 @@
 
 
 def kernel(unit, block, fblock, micro, len_s, x0_h, g_h, wu_h, wd_h, gu_h, gd_h,
-           xv, rv, w1v, w2v, own_u, own_v, in_u, in_v, sum_u, sum_v,
+           xv, rv, x_extra, w1v, w2v, own_u, own_v, in_u, in_v, sum_u, sum_v,
            rr_u, rr_v, rl_u, rl_v, out_u, out_v,
-           x_sem, r_sem, w_sem, f_sem, ds_sem, dr_sem,
+           x_sem, r_sem, w_sem, f_sem, t_send, t_recv, ds_sem, dr_sem,
            rs_u, rq_u, ls_u, lq_u, rs_v, rq_v, ls_v, lq_v,
            ou_sem, ov_sem, du_credit, dv_credit, ru_credit, lu_credit, rv_credit, lv_credit):
     toks, dim = x0_h.shape
     layers, _, ff = wu_h.shape
-    tiles = toks // block
     ftiles = toks // fblock
     piece = unit // PIECES
     wide = 2 * unit
@@ -52,6 +51,11 @@
     z = me // 2
     core = me % 2
     peer = z * 2 + (1 - core)
+    at_end = (z == 0) | (z == CHIPS - 1)
+    inward = jnp.where(z < CHIPS // 2, me + 2, me - 2)
+    outward = jnp.where(z < CHIPS // 2, me - 2, me + 2)
+    mine = jnp.where(at_end, ftiles - 1, ftiles + 1)
+    full = mine // 2
 
     def signal(sem, dev):
         pl.semaphore_signal(sem, inc=1, device_id={"fsdp": dev}, device_id_type=MESH)
@@ -94,9 +98,6 @@
                 wd_h.at[layer_of(m), span, :], w2v.at[slot, here, :], w_sem.at[slot, 2 + half]))
         return out
 
-    def rows_of(i):
-        return pl.ds(pl.multiple_of(i * block, block), block)
-
     def frows_of(i):
         return pl.ds(pl.multiple_of(i * fblock, fblock), fblock)
 
@@ -113,6 +114,21 @@
         row_ids = lax.broadcasted_iota(jnp.int32, r_val.shape, 0)
         rv[frows_of(i), :] = jnp.where(row_ids < left, r_val, jnp.zeros_like(r_val))
 
+    def tile_copies(dev):
+        src, dst = frows_of(ftiles - 1), frows_of(ftiles)
+        return (
+            remote(xv.at[src, :], xv.at[dst, :], t_send.at[0], t_recv.at[0], dev),
+            remote(rv.at[src, :], rv.at[dst, :], t_send.at[1], t_recv.at[1], dev),
+        )
+
+    def d_u(m):
+        slot = m % 2
+        return remote(own_u.at[slot, :, 1 - core], in_u.at[slot], ds_sem.at[0, slot], dr_sem.at[0, slot], peer)
+
+    def d_v(m):
+        slot = m % 2
+        return remote(own_v.at[slot, 1 - core], in_v.at[slot], ds_sem.at[1, slot], dr_sem.at[1, slot], peer)
+
     def forward(w1f, w2f, a_scr):
         width = ff // PARTS
 
@@ -121,24 +137,53 @@
             return pltpu.make_async_copy(wu_h.at[0, :, cols], w1f.at[:, cols], f_sem.at[part])
 
         w2_copy = pltpu.make_async_copy(wd_h.at[0], w2f, f_sem.at[PARTS])
-        for i in range(ftiles):
+        @pl.when(at_end)
+        def _():
+            x_copy(ftiles - 1).start()
+            r_copy(ftiles - 1).start()
+
+        for i in range(ftiles - 1):
             x_copy(i).start()
             if i == 0:
                 for part in range(PARTS):
                     w1_copy(part).start()
                 w2_copy.start()
-        for i in range(ftiles):
-            r_copy(i).start()
-
+                r_copy(0).start()
         for cp in w_copies(0):
             cp.start()
+        for i in range(1, ftiles - 1):
+            r_copy(i).start()
+
+        @pl.when(~at_end)
+        def _():
+            x_copy(ftiles - 1).start()
+            r_copy(ftiles - 1).start()
+
+        own_v[0] = jnp.zeros(own_v.shape[1:], F32)
         peers = 1 + jnp.where(z > 0, 1, 0) + jnp.where(z < CHIPS - 1, 1, 0)
         pl.semaphore_wait(barrier, peers)
 
+        @pl.when(at_end)
+        def _():
+            x_copy(ftiles - 1).wait()
+            r_copy(ftiles - 1).wait()
+            mask(ftiles - 1)
+            for cp in tile_copies(inward):
+                cp.start()
+
         def tile(i, first):
-            x_copy(i).wait()
-            r_copy(i).wait()
-            mask(i)
+            @pl.when(i < ftiles)
+            def _():
+                x_copy(i).wait()
+                r_copy(i).wait()
+                mask(i)
+
+            @pl.when(i == ftiles)
+            def _():
+                for cp in tile_copies(outward):
+                    cp.wait_recv()
+                x_extra[...] = xv[frows_of(i), :]
+
             x_val = xv[frows_of(i), :]
             for part in range(PARTS):
                 cols = slice(part * width, (part + 1) * width)
@@ -152,14 +197,27 @@
             if first:
                 w2_copy.wait()
             y_val = dot(a_scr[...], w2f[...], ((1,), (0,))).astype(BF16)
-            xv[frows_of(i), :] = (x_val.astype(F32) + y_val.astype(F32)).astype(BF16)
+            x1_val = (x_val.astype(F32) + y_val.astype(F32)).astype(BF16)
+            xv[frows_of(i), :] = x1_val
+            if first:
+                for cp in w_copies(0):
+                    cp.wait()
+            h_val = dot(x1_val, w1v[0], ((1,), (0,))).astype(BF16).astype(F32)
+            _, _, cdf = gelu_parts(h_val)
+            own_v[0] += dot((h_val * cdf).astype(BF16), rv[frows_of(i), :], ((0,), (0,))).reshape(own_v.shape[1:])
 
         def rest(i, carry):
             tile(i, False)
             return carry
 
         tile(0, True)
-        lax.fori_loop(1, ftiles, rest, 0)
+        lax.fori_loop(1, mine, rest, 0)
+        d_v(0).start()
+
+        @pl.when(at_end)
+        def _():
+            for cp in tile_copies(inward):
+                cp.wait_send()
 
     pl.run_scoped(
         forward,
@@ -167,19 +225,29 @@
 
     def backward(dxa):
         def clear(i, carry):
-            dxa[rows_of(i), :] = jnp.zeros((block, dim), F32)
+            dxa[frows_of(i), :] = jnp.zeros((fblock, dim), F32)
             return carry
 
-        lax.fori_loop(0, tiles, clear, 0)
-
-        def tile(m, i, back):
+        lax.fori_loop(0, mine, clear, 0)
+
+        def tile(m, i, back, short=False):
             slot = m % 2
-            rows = rows_of(i)
+            v_slot = jnp.where(m == 0, 1, slot)
+            rows = pl.ds(pl.multiple_of(i * block, block), fblock if short else block)
 
             @pl.when(m == per_layer)
             def _():
-                for k in range(block // fblock):
-                    x_copy(i * (block // fblock) + k).wait()
+                if short:
+                    @pl.when(at_end)
+                    def _():
+                        x_copy(2 * i).wait()
+
+                    @pl.when(~at_end)
+                    def _():
+                        xv[rows, :] = x_extra[...]
+                else:
+                    x_copy(2 * i).wait()
+                    x_copy(2 * i + 1).wait()
                 rv[rows, :] = (rv[rows, :].astype(F32) + dxa[rows, :]).astype(BF16)
 
             x_i, r_i = xv[rows, :], rv[rows, :]
@@ -189,17 +257,10 @@
             a_val = (h_val * cdf).astype(BF16)
             slope = cdf + (h_val * (0.5 - 0.5 * (th * th))) * (C1 + K3 * sq)
             dh_val = (da_val * slope).astype(BF16)
-            own_v[slot] += dot(a_val, r_i, ((0,), (0,))).reshape(own_v.shape[1:])
+            own_v[v_slot] += dot(a_val, r_i, ((0,), (0,))).reshape(own_v.shape[1:])
             own_u[slot] += dot(x_i, dh_val, ((0,), (0,))).reshape(own_u.shape[1:])
             if back:
                 dxa[rows, :] += dot(dh_val, w1v[slot], ((1,), (1,)))
-
-        def d_copies(m):
-            slot = m % 2
-            return (
-                remote(own_u.at[slot, :, 1 - core], in_u.at[slot], ds_sem.at[0, slot], dr_sem.at[0, slot], peer),
-                remote(own_v.at[slot, 1 - core], in_v.at[slot], ds_sem.at[1, slot], dr_sem.at[1, slot], peer),
-            )
 
         def far_first(zz, going):
             return list(range(CHIPS - 1, zz, -1)) if going > 0 else list(range(zz))
@@ -257,7 +318,7 @@
             blocks = far_first(zz, going) + ([] if first else [zz])
             pass_u(blocks[0])
             if not last:
-                @pl.when(beyond(m, zz, going))
+                @pl.when(beyond(m, zz, going) & (m > 0) if first else beyond(m, zz, going))
                 def _():
                     for p in range(PIECES):
                         if not first:
@@ -353,17 +414,34 @@
             lax.fori_loop(upto(k, n - 1), upto(k, n), one, 0)
 
         def add_cores(m):
-            for cp in d_copies(m):
-                cp.wait_recv()
+            d_u(m).wait_recv()
             sum_u[m % SLOTS] = own_u[m % 2, :, core] + in_u[m % 2]
+            d_u(m).wait_send()
+
+            @pl.when(m < total - 2)
+            def _():
+                signal(du_credit, peer)
+
+            @pl.when(m > 0)
+            def _():
+                add_cores_v(m)
+
+        def add_cores_v(m):
+            d_v(m).wait_recv()
             sum_v[m % SLOTS] = own_v[m % 2, core] + in_v[m % 2]
-            for cp in d_copies(m):
-                cp.wait_send()
+            d_v(m).wait_send()
 
             @pl.when(m < total - 2)
             def _():
-                signal(du_credit, peer)
                 signal(dv_credit, peer)
+
+        def first_rows():
+            add_cores_v(0)
+            for zz, going in ((0, 1), (CHIPS - 1, -1)):
+                @pl.when((z == zz) & beyond(0, zz, going))
+                def _():
+                    for p in range(PIECES):
+                        v_copy(0, p, going, True).start()
 
         def all_sums(n):
             turns(0, n, add_cores)
@@ -401,21 +479,32 @@
                     for cp in w_copies(n + 1):
                         cp.start()
 
-                for cp in w_copies(n):
-                    cp.wait()
+                @pl.when(n > 0)
+                def _():
+                    for cp in w_copies(n):
+                        cp.wait()
+
+                    own_v[n % 2] = jnp.zeros(own_v.shape[1:], F32)
+
+                @pl.when(n == 0)
+                def _():
+                    own_v[1] = jnp.zeros(own_v.shape[1:], F32)
 
                 own_u[n % 2] = jnp.zeros(own_u.shape[1:], F32)
-                own_v[n % 2] = jnp.zeros(own_v.shape[1:], F32)
 
                 @pl.when(n == per_layer)
                 def _():
-                    for i in range(ftiles):
+                    for i in range(ftiles - 1):
                         x_copy(i).start()
+
+                    @pl.when(~at_end)
+                    def _():
+                        x_copy(ftiles - 1).start()
 
 
             def half(phase, c):
                 lo = phase
-                hi = jnp.where(phase == 0, 1, tiles)
+                hi = jnp.where(phase == 0, 1, full)
 
                 def loop(cond, back):
                     @pl.when(cond)
@@ -426,6 +515,10 @@
 
                         lax.fori_loop(lo, hi, body, 0)
 
+                        @pl.when(phase == 1)
+                        def _():
+                            tile(n, full, back, True)
+
                 loop(run & (n < per_layer), True)
                 loop(run & (n >= per_layer), False)
 
@@ -436,10 +529,17 @@
                         pl.semaphore_wait(du_credit, 1)
                         pl.semaphore_wait(dv_credit, 1)
 
-                    for cp in d_copies(n):
-                        cp.start()
-
-                @pl.when(phase == 0)
+                    d_u(n).start()
+
+                    @pl.when(n > 0)
+                    def _():
+                        d_v(n).start()
+
+                @pl.when((phase == 0) & (n == 0))
+                def _():
+                    first_rows()
+
+                @pl.when((phase == 0) & (n > 0))
                 def _():
                     all_sums(n)
 
@@ -465,12 +565,13 @@
     rows_u = dim // (2 * CHIPS)
     wide = 2 * unit
     ftiles = toks // fblock
+    held = toks + fblock
     dma = pltpu.SemaphoreType.DMA
     vm = pltpu.VMEM
     u_blk = (CHIPS, rows_u, wide)
     v_blk = (unit, dim)
     scratch = [
-        vm((toks, dim), BF16), vm((toks, dim), BF16),
+        vm((held, dim), BF16), vm((held, dim), BF16), vm((fblock, dim), BF16),
         vm((2, dim, wide), BF16), vm((2, wide, dim), BF16),
         vm((2, CHIPS, 2, rows_u, wide), F32), vm((2, 2) + v_blk, F32),
         vm((2,) + u_blk, F32), vm((2,) + v_blk, F32),
@@ -478,7 +579,7 @@
         vm((SLOTS,) + u_blk, F32), vm((SLOTS,) + v_blk, F32),
         vm((SLOTS,) + u_blk, F32), vm((SLOTS,) + v_blk, F32),
         vm((2, rows_u, wide), F32), vm(v_blk, F32),
-        dma((ftiles,)), dma((ftiles,)), dma((2, 4)), dma((PARTS + 1,)), dma((2, 2)), dma((2, 2)),
+        dma((ftiles,)), dma((ftiles,)), dma((2, 4)), dma((PARTS + 1,)), dma((2,)), dma((2,)), dma((2, 2)), dma((2, 2)),
     ] + [dma((CHIPS, SLOTS))] * 4 + [dma((PIECES, SLOTS))] * 4 + [dma((2, 2)), dma] + [pltpu.SemaphoreType.REGULAR] * 6
     any_space = pl.BlockSpec(memory_space=pl.ANY)
     return pl.pallas_call(
@@ -491,7 +592,7 @@
         out_specs=[any_space] * 2,
         scratch_shapes=scratch,
         compiler_params=pltpu.CompilerParams(
-            collective_id=0, has_side_effects=True, vmem_limit_bytes=62 * 1024 * 1024),
+            collective_id=0, has_side_effects=True, vmem_limit_bytes=67_043_328),
         name="grads",
     )(lengths, x0, g, w_up, w_down)
 

time: 390 us -> 396 us (1.015)
  Pallas kernels: 384 us -> 390 us
    pallas_call x1, Pallas kernels: 384 us -> 390 us  [gradients(): pl.pallas_call(functools.partial(kernel, unit, block, fblock, micro), out...]
where the time goes in v3:
time: 396 us; the launch traced here: 395 us
  Pallas kernels  390 us (98%)
  local copies, waits for them, and re-layouts  4.86 us (1%)
    pallas_call x1, Pallas kernels, gradients(): pl.pallas_call(functools.partial(kernel, unit, block, fblock, micro), out...  390 us

profile of v3, /device:TPU:16, one launch (start us, length us, event | category | flops | bytes accessed | tf_op | source)
XLA Modules:
  0.0 395.5 jit_solution(8815723120843748388)
XLA Ops:
  0.6 390.0 %grads.1 = (f32[2,96,3072]{2,1,0:T(8,128)}, f32[2,384,768]{2,1,0:T(8,128)}) custom-call(s32[2]{0:T(128)} %bitcast.5, bf16[4096,768]{1,0:T(8,128)(2,1)} %bitcast.3, bf16[4096,768]{1,0:T(8,128)(2,1)} %bitcast.4, bf16[2,768,3072]{2,1,0:T(8,128)(2,1)} %wu_h.1, bf16[2,3072,768]{2,1,0:T(8,128)(2,1)} %wd_h.1), custom_call_target="tpu_custom_call" | custom-call | tf_op jit(solution)/shard_map/grads/pallas_call | solution.py:585
  390.6 0.0 copy-start
  390.6 3.4 copy.9
  394.1 0.0 copy-done
  394.1 1.4 copy.10
Async XLA Ops:
  390.6 3.5 copy-start

commit v4 on v3

--- a/solution.py
+++ b/solution.py
@@ -122,12 +122,10 @@
         )
 
     def d_u(m):
-        slot = m % 2
-        return remote(own_u.at[slot, :, 1 - core], in_u.at[slot], ds_sem.at[0, slot], dr_sem.at[0, slot], peer)
+        return remote(own_u.at[m % 2, :, 1 - core], in_u, ds_sem.at[0], dr_sem.at[0], peer)
 
     def d_v(m):
-        slot = m % 2
-        return remote(own_v.at[slot, 1 - core], in_v.at[slot], ds_sem.at[1, slot], dr_sem.at[1, slot], peer)
+        return remote(own_v.at[m % 2, 1 - core], in_v, ds_sem.at[1], dr_sem.at[1], peer)
 
     def forward(w1f, w2f, a_scr):
         width = ff // PARTS
@@ -159,7 +157,6 @@
             x_copy(ftiles - 1).start()
             r_copy(ftiles - 1).start()
 
-        own_v[0] = jnp.zeros(own_v.shape[1:], F32)
         peers = 1 + jnp.where(z > 0, 1, 0) + jnp.where(z < CHIPS - 1, 1, 0)
         pl.semaphore_wait(barrier, peers)
 
@@ -197,14 +194,7 @@
             if first:
                 w2_copy.wait()
             y_val = dot(a_scr[...], w2f[...], ((1,), (0,))).astype(BF16)
-            x1_val = (x_val.astype(F32) + y_val.astype(F32)).astype(BF16)
-            xv[frows_of(i), :] = x1_val
-            if first:
-                for cp in w_copies(0):
-                    cp.wait()
-            h_val = dot(x1_val, w1v[0], ((1,), (0,))).astype(BF16).astype(F32)
-            _, _, cdf = gelu_parts(h_val)
-            own_v[0] += dot((h_val * cdf).astype(BF16), rv[frows_of(i), :], ((0,), (0,))).reshape(own_v.shape[1:])
+            xv[frows_of(i), :] = (x_val.astype(F32) + y_val.astype(F32)).astype(BF16)
 
         def rest(i, carry):
             tile(i, False)
@@ -212,7 +202,6 @@
 
         tile(0, True)
         lax.fori_loop(1, mine, rest, 0)
-        d_v(0).start()
 
         @pl.when(at_end)
         def _():
@@ -232,7 +221,6 @@
 
         def tile(m, i, back, short=False):
             slot = m % 2
-            v_slot = jnp.where(m == 0, 1, slot)
             rows = pl.ds(pl.multiple_of(i * block, block), fblock if short else block)
 
             @pl.when(m == per_layer)
@@ -251,25 +239,29 @@
                 rv[rows, :] = (rv[rows, :].astype(F32) + dxa[rows, :]).astype(BF16)
 
             x_i, r_i = xv[rows, :], rv[rows, :]
+            da_val = dot(r_i, w2v[slot], ((1,), (1,)))
             h_val = dot(x_i, w1v[slot], ((1,), (0,))).astype(BF16).astype(F32)
-            da_val = dot(r_i, w2v[slot], ((1,), (1,)))
             sq, th, cdf = gelu_parts(h_val)
             a_val = (h_val * cdf).astype(BF16)
             slope = cdf + (h_val * (0.5 - 0.5 * (th * th))) * (C1 + K3 * sq)
             dh_val = (da_val * slope).astype(BF16)
-            own_v[v_slot] += dot(a_val, r_i, ((0,), (0,))).reshape(own_v.shape[1:])
-            own_u[slot] += dot(x_i, dh_val, ((0,), (0,))).reshape(own_u.shape[1:])
             if back:
                 dxa[rows, :] += dot(dh_val, w1v[slot], ((1,), (1,)))
+            own_u[slot] += dot(x_i, dh_val, ((0,), (0,))).reshape(own_u.shape[1:])
+            own_v[slot] += dot(a_val, r_i, ((0,), (0,))).reshape(own_v.shape[1:])
 
         def far_first(zz, going):
             return list(range(CHIPS - 1, zz, -1)) if going > 0 else list(range(zz))
+
+        def held(blk, going):
+            return blk - 1 if going > 0 else blk
 
         def u_copy(m, blk, going, first):
             slot = m % SLOTS
             dst, ssem, qsem = (rr_u, rs_u, rq_u) if going > 0 else (rl_u, ls_u, lq_u)
-            src = sum_u if first else dst
-            return remote(src.at[slot, blk], dst.at[slot, blk], ssem.at[blk, slot], qsem.at[blk, slot], me + 2 * going)
+            at = held(blk, going)
+            src = sum_u.at[slot, blk] if first else dst.at[slot, at]
+            return remote(src, dst.at[slot, at], ssem.at[blk, slot], qsem.at[blk, slot], me + 2 * going)
 
         def v_copy(m, p, going, first):
             slot = m % SLOTS
@@ -311,14 +303,14 @@
                 if not first:
                     u_copy(m, blk, going, False).wait_recv()
                     if blk != zz or keep:
-                        got_u[slot, blk] += sum_u[slot, blk]
+                        got_u[slot, held(blk, going)] += sum_u[slot, blk]
                 if blk != zz:
                     u_copy(m, blk, going, first).start()
 
             blocks = far_first(zz, going) + ([] if first else [zz])
             pass_u(blocks[0])
             if not last:
-                @pl.when(beyond(m, zz, going) & (m > 0) if first else beyond(m, zz, going))
+                @pl.when(beyond(m, zz, going))
                 def _():
                     for p in range(PIECES):
                         if not first:
@@ -365,8 +357,12 @@
                 for cp in out_copies_u(m - 2):
                     cp.wait()
 
-            one, two = terms(zz, sum_u, rr_u, rl_u)
-            out_u[m % 2] = one[slot, zz] + two[slot, zz]
+            parts = [sum_u[slot, zz]] if zz in (0, CHIPS - 1) else []
+            if zz > 0:
+                parts.append(rr_u[slot, held(zz, 1)])
+            if zz < CHIPS - 1:
+                parts.append(rl_u[slot, held(zz, -1)])
+            out_u[m % 2] = parts[0] + parts[1]
             for cp in out_copies_u(m):
                 cp.start()
 
@@ -415,33 +411,20 @@
 
         def add_cores(m):
             d_u(m).wait_recv()
-            sum_u[m % SLOTS] = own_u[m % 2, :, core] + in_u[m % 2]
+            sum_u[m % SLOTS] = own_u[m % 2, :, core] + in_u[...]
             d_u(m).wait_send()
 
-            @pl.when(m < total - 2)
+            @pl.when(m < total - 1)
             def _():
                 signal(du_credit, peer)
 
-            @pl.when(m > 0)
-            def _():
-                add_cores_v(m)
-
-        def add_cores_v(m):
             d_v(m).wait_recv()
-            sum_v[m % SLOTS] = own_v[m % 2, core] + in_v[m % 2]
+            sum_v[m % SLOTS] = own_v[m % 2, core] + in_v[...]
             d_v(m).wait_send()
 
-            @pl.when(m < total - 2)
+            @pl.when(m < total - 1)
             def _():
                 signal(dv_credit, peer)
-
-        def first_rows():
-            add_cores_v(0)
-            for zz, going in ((0, 1), (CHIPS - 1, -1)):
-                @pl.when((z == zz) & beyond(0, zz, going))
-                def _():
-                    for p in range(PIECES):
-                        v_copy(0, p, going, True).start()
 
         def all_sums(n):
             turns(0, n, add_cores)
@@ -479,17 +462,10 @@
                     for cp in w_copies(n + 1):
                         cp.start()
 
-                @pl.when(n > 0)
-                def _():
-                    for cp in w_copies(n):
-                        cp.wait()
-
-                    own_v[n % 2] = jnp.zeros(own_v.shape[1:], F32)
-
-                @pl.when(n == 0)
-                def _():
-                    own_v[1] = jnp.zeros(own_v.shape[1:], F32)
-
+                for cp in w_copies(n):
+                    cp.wait()
+
+                own_v[n % 2] = jnp.zeros(own_v.shape[1:], F32)
                 own_u[n % 2] = jnp.zeros(own_u.shape[1:], F32)
 
                 @pl.when(n == per_layer)
@@ -524,22 +500,15 @@
 
                 @pl.when(run & (phase == 1))
                 def _():
-                    @pl.when(n >= 2)
+                    @pl.when(n >= 1)
                     def _():
                         pl.semaphore_wait(du_credit, 1)
                         pl.semaphore_wait(dv_credit, 1)
 
                     d_u(n).start()
-
-                    @pl.when(n > 0)
-                    def _():
-                        d_v(n).start()
-
-                @pl.when((phase == 0) & (n == 0))
-                def _():
-                    first_rows()
-
-                @pl.when((phase == 0) & (n > 0))
+                    d_v(n).start()
+
+                @pl.when(phase == 0)
                 def _():
                     all_sums(n)
 
@@ -569,17 +538,18 @@
     dma = pltpu.SemaphoreType.DMA
     vm = pltpu.VMEM
     u_blk = (CHIPS, rows_u, wide)
+    line_blk = (CHIPS - 1, rows_u, wide)
     v_blk = (unit, dim)
     scratch = [
         vm((held, dim), BF16), vm((held, dim), BF16), vm((fblock, dim), BF16),
         vm((2, dim, wide), BF16), vm((2, wide, dim), BF16),
         vm((2, CHIPS, 2, rows_u, wide), F32), vm((2, 2) + v_blk, F32),
-        vm((2,) + u_blk, F32), vm((2,) + v_blk, F32),
+        vm(u_blk, F32), vm(v_blk, F32),
         vm((SLOTS,) + u_blk, F32), vm((SLOTS,) + v_blk, F32),
-        vm((SLOTS,) + u_blk, F32), vm((SLOTS,) + v_blk, F32),
-        vm((SLOTS,) + u_blk, F32), vm((SLOTS,) + v_blk, F32),
+        vm((SLOTS,) + line_blk, F32), vm((SLOTS,) + v_blk, F32),
+        vm((SLOTS,) + line_blk, F32), vm((SLOTS,) + v_blk, F32),
         vm((2, rows_u, wide), F32), vm(v_blk, F32),
-        dma((ftiles,)), dma((ftiles,)), dma((2, 4)), dma((PARTS + 1,)), dma((2,)), dma((2,)), dma((2, 2)), dma((2, 2)),
+        dma((ftiles,)), dma((ftiles,)), dma((2, 4)), dma((PARTS + 1,)), dma((2,)), dma((2,)), dma((2,)), dma((2,)),
     ] + [dma((CHIPS, SLOTS))] * 4 + [dma((PIECES, SLOTS))] * 4 + [dma((2, 2)), dma] + [pltpu.SemaphoreType.REGULAR] * 6
     any_space = pl.BlockSpec(memory_space=pl.ANY)
     return pl.pallas_call(
@@ -597,12 +567,47 @@
     )(lengths, x0, g, w_up, w_down)
 
 
+def hand_on_kernel(cuts, u_in, v_in, u_out, v_out, u_held, v_held, in_sem, out_sem):
+    jobs = []
+    for src, held, dst in ((v_in, v_held, v_out), (u_in, u_held, u_out)):
+        rows = src.shape[1] // cuts
+        for layer in range(src.shape[0]):
+            for cut in range(cuts):
+                part = pl.ds(cut * rows, rows)
+                k = len(jobs)
+                jobs.append((
+                    pltpu.make_async_copy(src.at[layer, part], held.at[layer, part], in_sem.at[k]),
+                    pltpu.make_async_copy(held.at[layer, part], dst.at[layer, part], out_sem.at[k])))
+    for get, _ in jobs:
+        get.start()
+    for get, put in jobs:
+        get.wait()
+        put.start()
+    for _, put in jobs:
+        put.wait()
+
+
+def hand_on(u, v, cuts=2):
+    any_space = pl.BlockSpec(memory_space=pl.ANY)
+    count = 2 * cuts * u.shape[0]
+    return pl.pallas_call(
+        functools.partial(hand_on_kernel, cuts),
+        out_shape=[jax.ShapeDtypeStruct(u.shape, F32), jax.ShapeDtypeStruct(v.shape, F32)],
+        in_specs=[any_space] * 2,
+        out_specs=[any_space] * 2,
+        scratch_shapes=[pltpu.VMEM(u.shape, F32), pltpu.VMEM(v.shape, F32),
+                        pltpu.SemaphoreType.DMA((count,)), pltpu.SemaphoreType.DMA((count,))],
+        compiler_params=pltpu.CompilerParams(vmem_limit_bytes=62 * 1024 * 1024),
+        name="hand_on",
+    )(u, v)
+
+
 def solution(mesh, block=1024, fblock=512, unit=128):
     def local_step(acts_in, cot_out, lengths, w_up, w_down):
         micro, tok_rows, dim = acts_in.shape
         x0 = acts_in.reshape(micro * tok_rows, dim)
         g = cot_out.reshape(micro * tok_rows, dim)
-        return gradients(x0, g, lengths.reshape(micro), w_up, w_down, block, fblock, unit)
+        return tuple(hand_on(*gradients(x0, g, lengths.reshape(micro), w_up, w_down, block, fblock, unit)))
 
     act_spec = P(None, ("part", "fsdp"), None)
     grad_spec = P("part", "fsdp", None)

time: 396 us -> 392 us (0.990)
  local copies, waits for them, and re-layouts: 4.86 us -> 0 us
    unnamed x4 -> x0, local copies, waits for them, and re-layouts: 4.86 us -> none
    pallas_call x0 -> x1, Pallas kernels: none -> 4.12 us  [hand_on(): pl.pallas_call(functools.partial(hand_on_kernel, cuts), out_shape=[jax.Sh...]
where the time goes in v4:
time: 392 us; the launch traced here: 391 us
  Pallas kernels  391 us (100%)
    pallas_call x1, Pallas kernels, gradients(): pl.pallas_call(functools.partial(kernel, unit, block, fblock, micro), out...  386 us

profile of v4, /device:TPU:16, one launch (start us, length us, event | category | flops | bytes accessed | tf_op | source)
XLA Modules:
  0.0 391.4 jit_solution(1583314715464548534)
XLA Ops:
  0.6 386.5 %grads.1 = (f32[2,96,3072]{2,1,0:T(8,128)}, f32[2,384,768]{2,1,0:T(8,128)}) custom-call(s32[2]{0:T(128)} %bitcast.5, bf16[4096,768]{1,0:T(8,128)(2,1)} %bitcast.3, bf16[4096,768]{1,0:T(8,128)(2,1)} %bitcast.4, bf16[2,768,3072]{2,1,0:T(8,128)(2,1)} %wu_h.1, bf16[2,3072,768]{2,1,0:T(8,128)(2,1)} %wd_h.1), custom_call_target="tpu_custom_call" | custom-call | tf_op jit(solution)/shard_map/grads/pallas_call | solution.py:555
  387.1 4.1 %hand_on.1 = (f32[2,96,3072]{2,1,0:T(8,128)}, f32[2,384,768]{2,1,0:T(8,128)}) custom-call(f32[2,96,3072]{2,1,0:T(8,128)} %get-tuple-element.4.u_in, f32[2,384,768]{2,1,0:T(8,128)} %get-tuple-element.5.v_in), custom_call_target="tpu_custom_call" | custom-call | tf_op jit(solution)/shard_map/hand_on/pallas_call | solution.py:593

commit v5 on v4

--- a/solution.py
+++ b/solution.py
@@ -33,13 +33,14 @@
 
 
 def kernel(unit, block, fblock, micro, len_s, x0_h, g_h, wu_h, wd_h, gu_h, gd_h,
-           xv, rv, x_extra, w1v, w2v, own_u, own_v, in_u, in_v, sum_u, sum_v,
+           xv, rv, w1v, w2v, own_u, own_v, in_u, in_v, sum_u, sum_v,
            rr_u, rr_v, rl_u, rl_v, out_u, out_v,
            x_sem, r_sem, w_sem, f_sem, t_send, t_recv, ds_sem, dr_sem,
            rs_u, rq_u, ls_u, lq_u, rs_v, rq_v, ls_v, lq_v,
            ou_sem, ov_sem, du_credit, dv_credit, ru_credit, lu_credit, rv_credit, lv_credit):
     toks, dim = x0_h.shape
     layers, _, ff = wu_h.shape
+    tiles = toks // block
     ftiles = toks // fblock
     piece = unit // PIECES
     wide = 2 * unit
@@ -55,7 +56,7 @@
     inward = jnp.where(z < CHIPS // 2, me + 2, me - 2)
     outward = jnp.where(z < CHIPS // 2, me - 2, me + 2)
     mine = jnp.where(at_end, ftiles - 1, ftiles + 1)
-    full = mine // 2
+    guest_turn = ftiles // 2
 
     def signal(sem, dev):
         pl.semaphore_signal(sem, inc=1, device_id={"fsdp": dev}, device_id_type=MESH)
@@ -114,12 +115,12 @@
         row_ids = lax.broadcasted_iota(jnp.int32, r_val.shape, 0)
         rv[frows_of(i), :] = jnp.where(row_ids < left, r_val, jnp.zeros_like(r_val))
 
-    def tile_copies(dev):
-        src, dst = frows_of(ftiles - 1), frows_of(ftiles)
-        return (
-            remote(xv.at[src, :], xv.at[dst, :], t_send.at[0], t_recv.at[0], dev),
-            remote(rv.at[src, :], rv.at[dst, :], t_send.at[1], t_recv.at[1], dev),
-        )
+    def guest_there(dev):
+        return remote(xv.at[frows_of(ftiles - 1), :], xv.at[frows_of(ftiles), :], t_send.at[0], t_recv.at[0], dev)
+
+    def guest_back(dev):
+        rows = frows_of(ftiles)
+        return remote(xv.at[rows, :], xv.at[rows, :], t_send.at[1], t_recv.at[1], dev)
 
     def d_u(m):
         return remote(own_u.at[m % 2, :, 1 - core], in_u, ds_sem.at[0], dr_sem.at[0], peer)
@@ -138,48 +139,43 @@
         @pl.when(at_end)
         def _():
             x_copy(ftiles - 1).start()
-            r_copy(ftiles - 1).start()
-
-        for i in range(ftiles - 1):
-            x_copy(i).start()
+
+        for i in range(ftiles):
+            if i < ftiles - 1:
+                x_copy(i).start()
             if i == 0:
                 for part in range(PARTS):
                     w1_copy(part).start()
                 w2_copy.start()
-                r_copy(0).start()
-        for cp in w_copies(0):
-            cp.start()
-        for i in range(1, ftiles - 1):
             r_copy(i).start()
 
         @pl.when(~at_end)
         def _():
             x_copy(ftiles - 1).start()
-            r_copy(ftiles - 1).start()
-
+
+        for cp in w_copies(0):
+            cp.start()
         peers = 1 + jnp.where(z > 0, 1, 0) + jnp.where(z < CHIPS - 1, 1, 0)
         pl.semaphore_wait(barrier, peers)
 
         @pl.when(at_end)
         def _():
             x_copy(ftiles - 1).wait()
-            r_copy(ftiles - 1).wait()
-            mask(ftiles - 1)
-            for cp in tile_copies(inward):
-                cp.start()
-
-        def tile(i, first):
-            @pl.when(i < ftiles)
+            guest_there(inward).start()
+
+        def tile(turn, first):
+            guest = ~at_end & (turn == guest_turn)
+            i = jnp.where(guest, ftiles, jnp.where(~at_end & (turn > guest_turn), turn - 1, turn))
+
+            @pl.when(guest)
+            def _():
+                guest_there(outward).wait_recv()
+
+            @pl.when(~guest)
             def _():
                 x_copy(i).wait()
                 r_copy(i).wait()
                 mask(i)
-
-            @pl.when(i == ftiles)
-            def _():
-                for cp in tile_copies(outward):
-                    cp.wait_recv()
-                x_extra[...] = xv[frows_of(i), :]
 
             x_val = xv[frows_of(i), :]
             for part in range(PARTS):
@@ -196,8 +192,12 @@
             y_val = dot(a_scr[...], w2f[...], ((1,), (0,))).astype(BF16)
             xv[frows_of(i), :] = (x_val.astype(F32) + y_val.astype(F32)).astype(BF16)
 
-        def rest(i, carry):
-            tile(i, False)
+            @pl.when(guest)
+            def _():
+                guest_back(outward).start()
+
+        def rest(turn, carry):
+            tile(turn, False)
             return carry
 
         tile(0, True)
@@ -205,8 +205,13 @@
 
         @pl.when(at_end)
         def _():
-            for cp in tile_copies(inward):
-                cp.wait_send()
+            guest_there(inward).wait_send()
+            r_copy(ftiles - 1).wait()
+            mask(ftiles - 1)
+
+        @pl.when(~at_end)
+        def _():
+            guest_back(outward).wait_send()
 
     pl.run_scoped(
         forward,
@@ -217,25 +222,23 @@
             dxa[frows_of(i), :] = jnp.zeros((fblock, dim), F32)
             return carry
 
-        lax.fori_loop(0, mine, clear, 0)
-
-        def tile(m, i, back, short=False):
+        lax.fori_loop(0, ftiles, clear, 0)
+
+        def tile(m, i, back):
             slot = m % 2
-            rows = pl.ds(pl.multiple_of(i * block, block), fblock if short else block)
+            rows = pl.ds(pl.multiple_of(i * block, block), block)
+
+            if back:
+                @pl.when((m == 0) & (i == tiles - 1) & at_end)
+                def _():
+                    guest_back(inward).wait_recv()
+                    xv[frows_of(ftiles - 1), :] = xv[frows_of(ftiles), :]
 
             @pl.when(m == per_layer)
             def _():
-                if short:
-                    @pl.when(at_end)
-                    def _():
-                        x_copy(2 * i).wait()
-
-                    @pl.when(~at_end)
-                    def _():
-                        xv[rows, :] = x_extra[...]
-                else:
-                    x_copy(2 * i).wait()
-                    x_copy(2 * i + 1).wait()
+                for k in range(block // fblock):
+                    x_copy(i * (block // fblock) + k).wait()
+
                 rv[rows, :] = (rv[rows, :].astype(F32) + dxa[rows, :]).astype(BF16)
 
             x_i, r_i = xv[rows, :], rv[rows, :]
@@ -470,17 +473,13 @@
 
                 @pl.when(n == per_layer)
                 def _():
-                    for i in range(ftiles - 1):
+                    for i in range(ftiles):
                         x_copy(i).start()
-
-                    @pl.when(~at_end)
-                    def _():
-                        x_copy(ftiles - 1).start()
 
 
             def half(phase, c):
                 lo = phase
-                hi = jnp.where(phase == 0, 1, full)
+                hi = jnp.where(phase == 0, 1, tiles)
 
                 def loop(cond, back):
                     @pl.when(cond)
@@ -491,10 +490,6 @@
 
                         lax.fori_loop(lo, hi, body, 0)
 
-                        @pl.when(phase == 1)
-                        def _():
-                            tile(n, full, back, True)
-
                 loop(run & (n < per_layer), True)
                 loop(run & (n >= per_layer), False)
 
@@ -524,7 +519,7 @@
                 cp.wait()
         out_copy_v(total - CHIPS).wait()
 
-    pl.run_scoped(backward, pltpu.VMEM(xv.shape, F32))
+    pl.run_scoped(backward, pltpu.VMEM(rv.shape, F32))
 
 
 def gradients(x0, g, lengths, w_up, w_down, block, fblock, unit):
@@ -541,7 +536,7 @@
     line_blk = (CHIPS - 1, rows_u, wide)
     v_blk = (unit, dim)
     scratch = [
-        vm((held, dim), BF16), vm((held, dim), BF16), vm((fblock, dim), BF16),
+        vm((held, dim), BF16), vm((toks, dim), BF16),
         vm((2, dim, wide), BF16), vm((2, wide, dim), BF16),
         vm((2, CHIPS, 2, rows_u, wide), F32), vm((2, 2) + v_blk, F32),
         vm(u_blk, F32), vm(v_blk, F32),

time: 392 us -> 385 us (0.982)
  Pallas kernels: 391 us -> 384 us
    pallas_call x1, Pallas kernels: 386 us -> 380 us  [gradients(): pl.pallas_call(functools.partial(kernel, unit, block, fblock, micro), out...]
where the time goes in v5:
time: 385 us
  Pallas kernels  384 us (100%)
    pallas_call x1, Pallas kernels, gradients(): pl.pallas_call(functools.partial(kernel, unit, block, fblock, micro), out...  380 us

profile of v5, /device:TPU:16, one launch (start us, length us, event | category | flops | bytes accessed | tf_op | source)
XLA Modules:
  0.0 384.7 jit_solution(16427068373760989381)
XLA Ops:
  0.6 379.7 %grads.1 = (f32[2,96,3072]{2,1,0:T(8,128)}, f32[2,384,768]{2,1,0:T(8,128)}) custom-call(s32[2]{0:T(128)} %bitcast.5, bf16[4096,768]{1,0:T(8,128)(2,1)} %bitcast.3, bf16[4096,768]{1,0:T(8,128)(2,1)} %bitcast.4, bf16[2,768,3072]{2,1,0:T(8,128)(2,1)} %wu_h.1, bf16[2,3072,768]{2,1,0:T(8,128)(2,1)} %wd_h.1), custom_call_target="tpu_custom_call" | custom-call | tf_op jit(solution)/shard_map/grads/pallas_call | solution.py:550
  380.4 4.1 %hand_on.1 = (f32[2,96,3072]{2,1,0:T(8,128)}, f32[2,384,768]{2,1,0:T(8,128)}) custom-call(f32[2,96,3072]{2,1,0:T(8,128)} %get-tuple-element.4.u_in, f32[2,384,768]{2,1,0:T(8,128)} %get-tuple-element.5.v_in), custom_call_target="tpu_custom_call" | custom-call | tf_op jit(solution)/shard_map/hand_on/pallas_call | solution.py:588

commit v6 on v5

--- a/solution.py
+++ b/solution.py
@@ -18,6 +18,7 @@
 CHIPS = 4
 HOP = 2
 SLOTS = 8
+CUTS = 4
 PIECES = 4
 PARTS = 4
 
@@ -234,12 +235,13 @@
                     guest_back(inward).wait_recv()
                     xv[frows_of(ftiles - 1), :] = xv[frows_of(ftiles), :]
 
-            @pl.when(m == per_layer)
-            def _():
-                for k in range(block // fblock):
-                    x_copy(i * (block // fblock) + k).wait()
-
-                rv[rows, :] = (rv[rows, :].astype(F32) + dxa[rows, :]).astype(BF16)
+            if not back:
+                @pl.when(m == per_layer)
+                def _():
+                    for k in range(block // fblock):
+                        x_copy(i * (block // fblock) + k).wait()
+
+                    rv[rows, :] = (rv[rows, :].astype(F32) + dxa[rows, :]).astype(BF16)
 
             x_i, r_i = xv[rows, :], rv[rows, :]
             da_val = dot(r_i, w2v[slot], ((1,), (1,)))
@@ -429,7 +431,7 @@
             def _():
                 signal(dv_credit, peer)
 
-        def all_sums(n):
+        def all_sums(n, drain):
             turns(0, n, add_cores)
             for zz in range(CHIPS):
                 @pl.when(z == zz)
@@ -439,7 +441,7 @@
                     def go(going):
                         turns(turn(zz, going), n, lambda m: flow(m, zz, going))
 
-                    if turn(zz, near) == 0:
+                    if not drain or turn(zz, near) == 0:
                         go(near)
                         go(far)
                     else:
@@ -455,64 +457,66 @@
 
                     turns(CHIPS - 1, n, lambda m: finish(m, zz))
 
-        def step(n, carry):
-            run = n < total
-
-            @pl.when(run)
-            def _():
-                @pl.when(n + 1 < total)
-                def _():
-                    for cp in w_copies(n + 1):
-                        cp.start()
-
-                for cp in w_copies(n):
-                    cp.wait()
-
-                own_v[n % 2] = jnp.zeros(own_v.shape[1:], F32)
-                own_u[n % 2] = jnp.zeros(own_u.shape[1:], F32)
-
+        def step(n, back):
+            @pl.when(n + 1 < total)
+            def _():
+                for cp in w_copies(n + 1):
+                    cp.start()
+
+            for cp in w_copies(n):
+                cp.wait()
+
+            own_u[n % 2] = jnp.zeros(own_u.shape[1:], F32)
+            own_v[n % 2] = jnp.zeros(own_v.shape[1:], F32)
+
+            if not back:
                 @pl.when(n == per_layer)
                 def _():
                     for i in range(ftiles):
                         x_copy(i).start()
 
-
-            def half(phase, c):
-                lo = phase
-                hi = jnp.where(phase == 0, 1, tiles)
-
-                def loop(cond, back):
-                    @pl.when(cond)
-                    def _():
-                        def body(i, cc):
-                            tile(n, i, back)
-                            return cc
-
-                        lax.fori_loop(lo, hi, body, 0)
-
-                loop(run & (n < per_layer), True)
-                loop(run & (n >= per_layer), False)
-
-                @pl.when(run & (phase == 1))
-                def _():
-                    @pl.when(n >= 1)
-                    def _():
-                        pl.semaphore_wait(du_credit, 1)
-                        pl.semaphore_wait(dv_credit, 1)
-
-                    d_u(n).start()
-                    d_v(n).start()
-
-                @pl.when(phase == 0)
-                def _():
-                    all_sums(n)
-
-                return c
-
-            lax.fori_loop(0, 2, half, 0)
-            return carry
-
-        lax.fori_loop(0, total + CHIPS, step, 0)
+            tile(n, 0, back)
+
+        def step_rest(n, back):
+            def rest(i, carry):
+                tile(n, i, back)
+                return carry
+
+            lax.fori_loop(1, tiles, rest, 0)
+
+            @pl.when(n >= 1)
+            def _():
+                pl.semaphore_wait(du_credit, 1)
+                pl.semaphore_wait(dv_credit, 1)
+
+            d_u(n).start()
+            d_v(n).start()
+
+        def back_step(n):
+            step(n, True)
+            all_sums(n, False)
+            step_rest(n, True)
+
+        def front_step(n):
+            @pl.when(n < total)
+            def _():
+                step(n, False)
+
+            all_sums(n, True)
+
+            @pl.when(n < total)
+            def _():
+                step_rest(n, False)
+
+        def steps(lo, hi, body):
+            def one(n, carry):
+                body(n)
+                return carry
+
+            lax.fori_loop(lo, hi, one, 0)
+
+        steps(0, per_layer, back_step)
+        steps(per_layer, total + CHIPS, front_step)
 
         for m in (total - 2, total - 1):
             for cp in out_copies_u(m):
@@ -582,7 +586,7 @@
         put.wait()
 
 
-def hand_on(u, v, cuts=2):
+def hand_on(u, v, cuts=CUTS):
     any_space = pl.BlockSpec(memory_space=pl.ANY)
     count = 2 * cuts * u.shape[0]
     return pl.pallas_call(

time: 385 us -> 385 us (level)
  no operation moved by 1% of the time
where the time goes in v6:
time: 385 us
  Pallas kernels  384 us (100%)
    pallas_call x1, Pallas kernels, gradients(): pl.pallas_call(functools.partial(kernel, unit, block, fblock, micro), out...  379 us

profile of v6, /device:TPU:16, one launch (start us, length us, event | category | flops | bytes accessed | tf_op | source)
XLA Modules:
  0.0 384.7 jit_solution(4370341132642697389)
XLA Ops:
  0.6 379.5 %grads.1 = (f32[2,96,3072]{2,1,0:T(8,128)}, f32[2,384,768]{2,1,0:T(8,128)}) custom-call(s32[2]{0:T(128)} %bitcast.5, bf16[4096,768]{1,0:T(8,128)(2,1)} %bitcast.3, bf16[4096,768]{1,0:T(8,128)(2,1)} %bitcast.4, bf16[2,768,3072]{2,1,0:T(8,128)(2,1)} %wu_h.1, bf16[2,3072,768]{2,1,0:T(8,128)(2,1)} %wd_h.1), custom_call_target="tpu_custom_call" | custom-call | tf_op jit(solution)/shard_map/grads/pallas_call | solution.py:554
  380.1 4.4 %hand_on.1 = (f32[2,96,3072]{2,1,0:T(8,128)}, f32[2,384,768]{2,1,0:T(8,128)}) custom-call(f32[2,96,3072]{2,1,0:T(8,128)} %get-tuple-element.4.u_in, f32[2,384,768]{2,1,0:T(8,128)} %get-tuple-element.5.v_in), custom_call_target="tpu_custom_call" | custom-call | tf_op jit(solution)/shard_map/hand_on/pallas_call | solution.py:592

commit v7 on v5

--- a/solution.py
+++ b/solution.py
@@ -286,14 +286,14 @@
         def keeps(zz, going):
             return 2 * turn(zz, going) < CHIPS - 1
 
-        def flow(m, zz, going):
+        def flow(m, zz, going, parts=(True, True)):
             slot = m % SLOTS
             first, last = ends(zz, going)
             keep = keeps(zz, going)
             got_u, credit_u = (rr_u, ru_credit) if going > 0 else (rl_u, lu_credit)
             got_v, credit_v = (rr_v, rv_credit) if going > 0 else (rl_v, lv_credit)
 
-            if not last:
+            if not last and parts[0]:
                 @pl.when(m >= SLOTS)
                 def _():
                     pl.semaphore_wait(credit_u, 1)
@@ -311,8 +311,9 @@
                     u_copy(m, blk, going, first).start()
 
             blocks = far_first(zz, going) + ([] if first else [zz])
-            pass_u(blocks[0])
-            if not last:
+            if parts[0]:
+                pass_u(blocks[0])
+            if not last and parts[0]:
                 @pl.when(beyond(m, zz, going))
                 def _():
                     for p in range(PIECES):
@@ -322,7 +323,7 @@
                             got_v[slot, part] += sum_v[slot, part]
                         v_copy(m, p, going, first).start()
 
-            if not first:
+            if not first and parts[0]:
                 @pl.when(owner_of(m) == zz)
                 def _():
                     for p in range(PIECES):
@@ -330,7 +331,7 @@
                     if keep:
                         got_v[slot] += sum_v[slot]
 
-            for blk in blocks[1:]:
+            for blk in blocks[1:] if parts[1] else ():
                 pass_u(blk)
 
         def out_copies_u(m):
@@ -405,12 +406,12 @@
             draining = jnp.where(late < k, total + 1 - HOP * (k - late), total)
             return jnp.maximum(jnp.where(n < total, n - HOP * k, draining), 0)
 
-        def turns(k, n, body):
+        def turns(k, n, body, limit=total):
             def one(m, carry):
                 body(m)
                 return carry
 
-            lax.fori_loop(upto(k, n - 1), upto(k, n), one, 0)
+            lax.fori_loop(upto(k, n - 1), jnp.minimum(upto(k, n), limit), one, 0)
 
         def add_cores(m):
             d_u(m).wait_recv()
@@ -436,22 +437,35 @@
                 def _():
                     near, far = sorted((1, -1), key=lambda going: turn(zz, going))
 
-                    def go(going):
-                        turns(turn(zz, going), n, lambda m: flow(m, zz, going))
-
-                    if turn(zz, near) == 0:
-                        go(near)
-                        go(far)
+                    k_near, k_far = turn(zz, near), turn(zz, far)
+                    end = total if k_near == 0 else total - 1
+
+                    def go(going, k):
+                        turns(k, n, lambda m: flow(m, zz, going), end)
+
+                    if k_near == 0:
+                        go(near, k_near)
+                        go(far, k_far)
                     else:
                         @pl.when(n < total)
                         def _():
-                            go(near)
-
-                        go(far)
+                            go(near, k_near)
+
+                        go(far, k_far)
 
                         @pl.when(n >= total)
                         def _():
-                            go(near)
+                            go(near, k_near)
+
+                        @pl.when(n == total + k_near)
+                        def _():
+                            flow(end, zz, near, (True, False))
+                            flow(end, zz, far, (True, False))
+                            flow(end, zz, near, (False, True))
+
+                        @pl.when(n == total + k_far)
+                        def _():
+                            flow(end, zz, far, (False, True))
 
                     turns(CHIPS - 1, n, lambda m: finish(m, zz))
 

time: 385 us -> 388 us (level)
  no operation moved by 1% of the time
where the time goes in v7:
time: 388 us; the launch traced here: 385 us
  Pallas kernels  384 us (99%)
    pallas_call x1, Pallas kernels, gradients(): pl.pallas_call(functools.partial(kernel, unit, block, fblock, micro), out...  380 us

profile of v7, /device:TPU:16, one launch (start us, length us, event | category | flops | bytes accessed | tf_op | source)
XLA Modules:
  0.0 384.7 jit_solution(6705212278239799989)
XLA Ops:
  0.6 379.8 %grads.1 = (f32[2,96,3072]{2,1,0:T(8,128)}, f32[2,384,768]{2,1,0:T(8,128)}) custom-call(s32[2]{0:T(128)} %bitcast.5, bf16[4096,768]{1,0:T(8,128)(2,1)} %bitcast.3, bf16[4096,768]{1,0:T(8,128)(2,1)} %bitcast.4, bf16[2,768,3072]{2,1,0:T(8,128)(2,1)} %wu_h.1, bf16[2,3072,768]{2,1,0:T(8,128)(2,1)} %wd_h.1), custom_call_target="tpu_custom_call" | custom-call | tf_op jit(solution)/shard_map/grads/pallas_call | solution.py:564
  380.4 4.1 %hand_on.1 = (f32[2,96,3072]{2,1,0:T(8,128)}, f32[2,384,768]{2,1,0:T(8,128)}) custom-call(f32[2,96,3072]{2,1,0:T(8,128)} %get-tuple-element.4.u_in, f32[2,384,768]{2,1,0:T(8,128)} %get-tuple-element.5.v_in), custom_call_target="tpu_custom_call" | custom-call | tf_op jit(solution)/shard_map/hand_on/pallas_call | solution.py:602
